TPU v7x, 32 devices: a whole 2x2x4 slice. The times are simulated.
32 devices in a mesh: section: 2 (over x), view: 8 (over z, y), scene: 2 (over core).
Axes of the slice: x: 2, y: 2, z: 4, core: 2. Of those that a mesh axis runs over, the one named last changes fastest.
Arguments:
- tokens: bfloat16 [2, 512, 1024], P('scene', ('section', 'view')), may hold values from -6 to 6
- norm_gain: float32 [1024], replicated, may hold values from 0.1 to 1.9
- head_weight: bfloat16 [1024, 512], replicated, may hold values from -0.1875 to 0.1875
- tile_lists: int32 [2, 64, 128], P('scene', ('section', 'view')), may hold values from 0 to 32767, as said below
- tile_counts: int32 [2, 64], P('scene', ('section', 'view')), may hold values from 1 to 128, as said below
- cameras: float32 [2, 2, 8], P('scene'), may hold values from -3 to 3
- targets: bfloat16 [2, 64, 768], P('scene', ('section', 'view')), may hold values from 0 to 1
Outputs:
- image: bfloat16 [2, 64, 768], P('scene', ('section', 'view'))
- grad_head: float32 [1024, 512], replicated
- loss: float32 [], replicated
Inputs may be any that keep to these rules, and one draw needn't show every extreme that they name: `tile_lists`: gaussian n of a scene has owner n // 2048. Among the 512 slots (live or not) of each aligned block of 4 tiles, at most 64 name Gaussians of one owner, and in every such block some owner is named exactly 64 times. `tile_counts`: the first tile of each scene has 128 live slots.
All inputs are finite; a program needn't handle non-finite values.
Results may differ from a plain program's by a relative error of at most 0.014.
Values may be sent and summed in bfloat16 or wider, within the bound.
A program may use at most 256 MiB of HBM per device.

v0:
```python
import functools

import jax
import jax.numpy as jnp
from jax import lax
from jax.experimental import pallas as pl
from jax.experimental.pallas import tpu as pltpu
from jax.sharding import PartitionSpec as P

PARAMS = 8
SIDE = 16
VIEWS = 2
MESH = pl.DeviceIdType.MESH
F32 = jnp.float32
BF16 = jnp.bfloat16
NN = (((1,), (0,)), ((), ()))
NT = (((1,), (1,)), ((), ()))
TN = (((0,), (0,)), ((), ()))


def mm(a, b, dims):
    return lax.dot_general(a, b, dims, preferred_element_type=F32)


def split(x):
    hi = x.astype(BF16)
    lo = (x - hi.astype(F32)).astype(BF16)
    return hi, lo


def mm2(a, x, dims):
    hi, lo = split(x)
    return mm(a, hi, dims) + mm(a, lo, dims)


def mm3(x, y, dims):
    xh, xl = split(x)
    yh, yl = split(y)
    return mm(xh, yh, dims) + mm(xh, yl, dims) + mm(xl, yh, dims)


def sigmoid(x):
    return 1.0 / (1.0 + jnp.exp(-x))


def pick(row, tokens, gpt):
    tok = row // gpt
    at = lax.broadcasted_iota(jnp.int32, (tokens, row.shape[1]), 0)
    return jnp.where(at == tok, 1.0, 0.0).astype(BF16)


def kernel(
    nsec, nview, factor,
    tok_ref, gain_ref, w_ref, list_ref, count_ref, cam_ref, want_ref,
    image_ref, grad_ref, loss_ref,
    heads, norms, lists, grads, dhead, mine, theirs, loss_mine, loss_theirs,
    s_list, r_list, s_head, r_head, s_norm, r_norm, s_grad, r_grad, s_part, r_part, s_loss, r_loss,
):
    group = nsec * nview
    sec, view, scene = lax.axis_index("section"), lax.axis_index("view"), lax.axis_index("scene")
    me = sec * nview + view
    tok_rows, width = tok_ref.shape
    outw = w_ref.shape[1]
    gpt = outw // PARAMS
    tiles, K = list_ref.shape
    tokens = group * tok_rows
    pix = SIDE * SIDE

    def peer(i):
        j = lax.rem(me + i, group)
        return j, (j // nview, lax.rem(j, nview), scene)

    def along_view(i):
        v = lax.rem(view + i, nview)
        return sec * nview + v, (sec, v, scene)

    def along_section(i):
        s = lax.rem(sec + i, nsec)
        return s, (s, view, scene)

    partner = (sec, view, 1 - scene)

    barrier = pltpu.get_barrier_semaphore()

    @pl.loop(1, group)
    def _(i):
        pl.semaphore_signal(barrier, inc=1, device_id=peer(i)[1], device_id_type=MESH)

    pl.semaphore_signal(barrier, inc=1, device_id=partner, device_id_type=MESH)

    x = tok_ref[...].astype(F32)
    scale = lax.rsqrt(jnp.mean(x * x, axis=-1, keepdims=True) + 1e-06)
    normed = (x * scale * gain_ref[...]).astype(BF16)
    norms[me] = normed
    heads[me] = mm(normed, w_ref[...], NN).astype(BF16)
    lists[me] = list_ref[...]

    pl.semaphore_wait(barrier, group)

    def push(buf, src, send, recv, i):
        j, where = peer(i)
        return pltpu.make_async_remote_copy(
            src_ref=src, dst_ref=buf.at[me], send_sem=send.at[i], recv_sem=recv.at[me],
            device_id=where, device_id_type=MESH,
        )

    def take(buf, send, recv, j):
        pltpu.make_async_remote_copy(
            src_ref=buf.at[j], dst_ref=buf.at[j], send_sem=send.at[0], recv_sem=recv.at[j],
            device_id=partner, device_id_type=MESH,
        ).wait_recv()

    def take_all(buf, send, recv):
        @pl.loop(1, group)
        def _(i):
            take(buf, send, recv, peer(i)[0])

    def first(buf, send, recv, i):
        return pltpu.make_async_remote_copy(
            src_ref=buf.at[me], dst_ref=buf.at[me], send_sem=send.at[i], recv_sem=recv.at[me],
            device_id=along_view(i)[1], device_id_type=MESH,
        )

    def relay(buf, send, recv, i, k):
        j = along_view(i)[0]
        return pltpu.make_async_remote_copy(
            src_ref=buf.at[j], dst_ref=buf.at[j],
            send_sem=send.at[nview + i * (nsec - 1) + k - 1], recv_sem=recv.at[j],
            device_id=along_section(k)[1], device_id_type=MESH,
        )

    def spread_own(buf, send, recv):
        for k in range(1, nsec):
            relay(buf, send, recv, 0, k).start()

        @pl.loop(1, nview)
        def _(i):
            first(buf, send, recv, i).start()

    def spread_rest(buf, send, recv):
        @pl.loop(1, nview)
        def _(i):
            take(buf, send, recv, along_view(i)[0])
            for k in range(1, nsec):
                relay(buf, send, recv, i, k).start()

    def collect(buf, send, recv):
        for k in range(1, nsec):
            s = along_section(k)[0]

            @pl.loop(0, nview)
            def _(i):
                take(buf, send, recv, s * nview + lax.rem(view + i, nview))

    def drain(buf, send, recv):
        @pl.loop(1, nview)
        def _(i):
            first(buf, send, recv, i).wait_send()

        @pl.loop(0, nview)
        def _(i):
            for k in range(1, nsec):
                relay(buf, send, recv, i, k).wait_send()

    @pl.loop(1, group)
    def _(i):
        push(lists, list_ref, s_list, r_list, i).start()

    spread_own(heads, s_head, r_head)

    own = jnp.concatenate([list_ref[pl.ds(b, 1), :] for b in range(tiles)], axis=1)
    hot = pick(own, tokens, gpt)
    inner = own - (own // gpt) * gpt
    at_g = lax.broadcasted_iota(jnp.int32, (gpt, tiles * K), 0)
    mask = jnp.where(at_g == inner, 1.0, 0.0)

    spread_rest(heads, s_head, r_head)
    collect(heads, s_head, r_head)
    spread_own(norms, s_norm, r_norm)
    table = heads[...].reshape(tokens, outw)
    picked = mm(table, hot, TN)
    rows = [
        jnp.sum(picked[p * gpt : (p + 1) * gpt] * mask, axis=0, keepdims=True)
        for p in range(PARAMS)
    ]

    place = lax.broadcasted_iota(jnp.int32, (1, pix), 1)
    across = ((place % SIDE).astype(F32) + 0.5) * (2.0 / SIDE) - 1.0
    down = ((place // SIDE).astype(F32) + 0.5) * (2.0 / SIDE) - 1.0
    ka = lax.broadcasted_iota(jnp.int32, (K, K), 0)
    kb = lax.broadcasted_iota(jnp.int32, (K, K), 1)
    lower = jnp.where(kb < ka, 1.0, 0.0).astype(BF16)
    upper = jnp.where(kb > ka, 1.0, 0.0).astype(BF16)
    ones = jnp.ones((8, pix), BF16)
    per_view = (tiles * group) // VIEWS
    slot = lax.broadcasted_iota(jnp.int32, (1, K), 1)
    zero_row = jnp.zeros((1, K), F32)

    for b in range(tiles):
        cut = slice(b * K, (b + 1) * K)
        mx, my, mz, ls, op, cr, cg, cb = [r[:, cut] for r in rows]
        vi = (me * tiles + b) // per_view
        cam = [cam_ref[vi, n] for n in range(8)]
        live = jnp.where(slot < count_ref[b], 1.0, 0.0)
        sx = jnp.tanh(cam[0] * mx + cam[1] * my + cam[2] * mz + cam[3])
        sy = jnp.tanh(cam[4] * mx + cam[5] * my + cam[6] * mz + cam[7])
        spread = jnp.exp(-2.0 * ls)
        sop = sigmoid(op)
        amp = 0.3 * sop * live
        shade = sigmoid(jnp.concatenate([cr, cg, cb], axis=0))
        shade8 = jnp.concatenate([shade, jnp.zeros((5, K), F32)], axis=0)
        cols = jnp.concatenate([sx, sy, spread, amp, jnp.zeros((K - 4, K), F32)], axis=0).T
        csx, csy, csp, camp = [cols[:, n : n + 1] for n in range(4)]
        dx = across - csx
        dy = down - csy
        r2 = dx * dx + dy * dy
        alpha = camp * jnp.exp(-0.5 * r2 * csp)
        rest = 1.0 - alpha
        trans = jnp.exp(mm2(lower, jnp.log(rest), NN))
        weight = alpha * trans
        colour = mm3(shade8, weight, NN)
        for c in range(3):
            image_ref[pl.ds(b, 1), c * pix : (c + 1) * pix] = colour[c : c + 1].astype(BF16)
        want = jnp.concatenate(
            [want_ref[pl.ds(b, 1), c * pix : (c + 1) * pix].astype(F32) for c in range(3)]
            + [jnp.zeros((5, pix), F32)],
            axis=0,
        )
        diff = colour - want
        sq = jnp.sum(diff * diff, axis=0, keepdims=True)
        part = sq[:, :K]
        for n in range(1, pix // K):
            part = part + sq[:, n * K : (n + 1) * K]
        part = part * factor
        dcol = (2.0 * factor) * diff
        dw = mm3(shade8, dcol, TN)
        dshade = mm3(dcol, weight, NT)
        dww = dw * weight
        dlogs = mm2(upper, dww, NN)
        h = dww - dlogs * alpha / rest
        s_h = mm2(ones, h, NT)[0:1]
        s_x = mm2(ones, h * dx, NT)[0:1]
        s_y = mm2(ones, h * dy, NT)[0:1]
        s_r = mm2(ones, h * r2, NT)[0:1]
        px = spread * s_x * (1.0 - sx * sx)
        py = spread * s_y * (1.0 - sy * sy)
        dcolour = dshade[0:3] * shade * (1.0 - shade)
        l0 = part.astype(BF16).astype(F32)
        l1 = (part - l0).astype(BF16).astype(F32)
        l2 = part - l0 - l1
        out = jnp.concatenate(
            [
                cam[0] * px + cam[4] * py,
                cam[1] * px + cam[5] * py,
                cam[2] * px + cam[6] * py,
                spread * s_r,
                (1.0 - sop) * s_h,
                dcolour,
                l0,
                l1,
                l2,
                jnp.zeros((5, K), F32),
            ],
            axis=0,
        )
        grads[me, :, cut] = out.astype(BF16)

    @pl.loop(1, group)
    def _(i):
        push(grads, grads.at[me], s_grad, r_grad, i).start()

    spread_rest(norms, s_norm, r_norm)
    take_all(lists, s_list, r_list)
    dhead[...] = jnp.zeros_like(dhead)
    loss_mine[...] = jnp.zeros_like(loss_mine)

    @pl.loop(0, group)
    def _(j):
        row = jnp.concatenate([lists[j, pl.ds(b, 1), :] for b in range(tiles)], axis=1)
        where = pick(row, tokens, gpt)
        g = row - (row // gpt) * gpt
        fits = lax.broadcasted_iota(jnp.int32, (gpt, tiles * K), 0) == g

        @pl.when(j != me)
        def _():
            take(grads, s_grad, r_grad, j)

        got = grads[j].astype(F32)
        spreadout = jnp.concatenate(
            [jnp.where(fits, got[p : p + 1], 0.0).astype(BF16) for p in range(PARAMS)], axis=0
        )
        dhead[...] += mm(where, spreadout, NT)
        lossy = got[8:9] + got[9:10] + got[10:11]
        for b in range(tiles):
            loss_mine[0:1, :] += lossy[:, b * K : (b + 1) * K]

    collect(norms, s_norm, r_norm)
    loss_copy = pltpu.make_async_remote_copy(
        src_ref=loss_mine, dst_ref=loss_theirs, send_sem=s_loss, recv_sem=r_loss,
        device_id=partner, device_id_type=MESH,
    )
    dh = dhead[...].astype(BF16)
    dhead_rows = 256
    chunks = width // dhead_rows

    def part_copy(n):
        span = pl.ds(n * dhead_rows, dhead_rows)
        return pltpu.make_async_remote_copy(
            src_ref=mine.at[span], dst_ref=theirs.at[span],
            send_sem=s_part.at[n], recv_sem=r_part.at[n],
            device_id=partner, device_id_type=MESH,
        )

    for n in range(chunks):
        a = norms[:, :, n * dhead_rows : (n + 1) * dhead_rows].reshape(tokens, dhead_rows)
        mine[n * dhead_rows : (n + 1) * dhead_rows, :] = mm(a, dh, TN).astype(BF16)
        if n == 0:
            loss_copy.start()
        else:
            part_copy(n - 1).start()
    part_copy(chunks - 1).start()

    for n in range(chunks):
        part_copy(n).wait_recv()
        span = slice(n * dhead_rows, (n + 1) * dhead_rows)
        grad_ref[span, :] = (mine[span, :].astype(F32) + theirs[span, :].astype(F32)).astype(BF16)
    loss_copy.wait_recv()
    loss_ref[...] = jnp.broadcast_to(
        jnp.sum(loss_mine[...] + loss_theirs[...], keepdims=True), loss_ref.shape
    )

    loss_copy.wait_send()
    for n in range(chunks):
        part_copy(n).wait_send()

    @pl.loop(1, group)
    def _(i):
        push(lists, list_ref, s_list, r_list, i).wait_send()
        push(grads, grads.at[me], s_grad, r_grad, i).wait_send()

    drain(heads, s_head, r_head)
    drain(norms, s_norm, r_norm)


def solution(mesh):
    nsec, nview, nscene = mesh.shape["section"], mesh.shape["view"], mesh.shape["scene"]
    group = nsec * nview

    def body(tokens, norm_gain, head_weight, tile_lists, tile_counts, cameras, targets):
        tok_rows, width = tokens.shape[1:]
        outw = head_weight.shape[1]
        tiles, K = tile_lists.shape[1:]
        factor = 1.0 / (nscene * tiles * group)
        vmem = pl.BlockSpec(memory_space=pltpu.VMEM)
        smem = pl.BlockSpec(memory_space=pltpu.SMEM)
        dma = pltpu.SemaphoreType.DMA
        image, grad, loss = pl.pallas_call(
            functools.partial(kernel, nsec, nview, factor),
            out_shape=(
                jax.ShapeDtypeStruct((tiles, targets.shape[2]), BF16),
                jax.ShapeDtypeStruct((width, outw), BF16),
                jax.ShapeDtypeStruct((8, 128), F32),
            ),
            in_specs=[vmem, vmem, vmem, vmem, smem, smem, vmem],
            out_specs=(vmem, vmem, vmem),
            scratch_shapes=[
                pltpu.VMEM((group, tok_rows, outw), BF16),
                pltpu.VMEM((group, tok_rows, width), BF16),
                pltpu.VMEM((group, tiles, K), jnp.int32),
                pltpu.VMEM((group, 16, tiles * K), BF16),
                pltpu.VMEM((group * tok_rows, outw), F32),
                pltpu.VMEM((width, outw), BF16),
                pltpu.VMEM((width, outw), BF16),
                pltpu.VMEM((8, K), F32),
                pltpu.VMEM((8, K), F32),
            ]
            + [dma((group,))] * 2
            + [dma((nview * nsec,)), dma((group,))] * 2
            + [dma((group,))] * 2
            + [dma((width // 256,))] * 2
            + [dma, dma],
            compiler_params=pltpu.CompilerParams(
                collective_id=0, has_side_effects=True, vmem_limit_bytes=60 * 1024 * 1024
            ),
        )(
            tokens[0], norm_gain[None], head_weight, tile_lists[0], tile_counts[0], cameras[0],
            targets[0],
        )
        return image[None], grad.astype(F32), loss[0, 0]

    in_specs = (
        P("scene", ("section", "view"), None),
        P(),
        P(),
        P("scene", ("section", "view"), None),
        P("scene", ("section", "view")),
        P("scene", None, None),
        P("scene", ("section", "view"), None),
    )
    out_specs = (P("scene", ("section", "view"), None), P(), P())
    return jax.shard_map(body, mesh=mesh, in_specs=in_specs, out_specs=out_specs, check_vma=False)
```

profile of v0, /device:TPU:27, one launch (start us, length us, event | category | flops | bytes accessed | tf_op | source)
XLA Modules:
  0.0 57.7 jit_solution(7469781707545154565)
XLA Ops:
  0.6 52.4 %shard_map.94 = (bf16[4,768]{1,0:T(4,128)(2,1)}, bf16[1024,512]{1,0:T(8,128)(2,1)}, f32[8,128]{1,0:T(8,128)}) custom-call(bf16[32,1024]{1,0:T(8,128)(2,1)} %bitcast.8, f32[1,1024]{1,0:T(1,128)} %bitcast.11, bf16[1024,512]{1,0:T(8,128)(2,1)} %w_ref.1, s32[4,128]{1,0:T(4,128)} %bitcast.12, s32[4]{0:T(128)} %bitcast.14, f32[2,8]{1,0:T(2,128)} %bitcast.13, ...), custom_call_target="tpu_custom_call" | custom-call | tf_op jit(solution)/shard_map/pallas_call | solution.py:357
  53.0 0.0 copy-start
  53.0 1.2 %slice.3 = f32[1,1]{1,0:T(1,128)} slice(f32[8,128]{1,0:T(8,128)} %get-tuple-element.8), slice={[0:1], [0:1]} | slice | bytes 8 | tf_op jit(solution)/shard_map/slice | solution.py:389
  54.2 2.8 %convert_element_type.3 = f32[1024,512]{1,0:T(8,128)} convert(bf16[1024,512]{1,0:T(8,128)(2,1)} %get-tuple-element.7) | non-fusion elementwise | flops 524288 | bytes 3145728 | tf_op jit(solution)/shard_map/convert_element_type | solution.py:389
  57.1 0.0 copy-done
  57.1 0.6 %copy.11 = bf16[1,4,768]{2,1,0:T(4,128)(2,1)} copy(bf16[1,4,768]{2,1,0:T(4,128)(2,1)S(1)} %bitcast.10) | data formatting | bytes 12288
Async XLA Ops:
  53.0 4.0 %copy-start = (bf16[4,768]{1,0:T(4,128)(2,1)S(1)}, bf16[4,768]{1,0:T(4,128)(2,1)}, u32[]{:S(2)}) copy-start(bf16[4,768]{1,0:T(4,128)(2,1)} %get-tuple-element.6) | copy-start | bytes 18436
where the time goes:
time: 57.9 us; the launch traced here: 57.7 us
  Pallas kernels  52.4 us (91%)
  other arithmetic  2.83 us (5%)
  local copies, waits for them, and re-layouts  1.79 us (3%)
  between operations  0.65 us (1%)
    pallas_call x1, Pallas kernels, body(): pl.pallas_call(functools.partial(kernel, nsec, nview, factor), out_shape=...  52.4 us
    convert_element_type x1, other arithmetic, body(): return (image[None], grad.astype(F32), loss[0, 0])  2.83 us
    slice x1, local copies, waits for them, and re-layouts, body(): return (image[None], grad.astype(F32), loss[0, 0])  1.2 us

commit v1 on v0

v1 whole, which is shorter than its diff:
```python
import functools

import jax
import jax.numpy as jnp
from jax import lax
from jax.experimental import pallas as pl
from jax.experimental.pallas import tpu as pltpu
from jax.sharding import PartitionSpec as P

PARAMS = 8
SIDE = 16
VIEWS = 2
MESH = pl.DeviceIdType.MESH
F32 = jnp.float32
BF16 = jnp.bfloat16
NN = (((1,), (0,)), ((), ()))
NT = (((1,), (1,)), ((), ()))
TN = (((0,), (0,)), ((), ()))


def mm(a, b, dims):
    return lax.dot_general(a, b, dims, preferred_element_type=F32)


def split(x):
    hi = x.astype(BF16)
    lo = (x - hi.astype(F32)).astype(BF16)
    return hi, lo


def mm2(a, x, dims):
    hi, lo = split(x)
    return mm(a, hi, dims) + mm(a, lo, dims)


def mm3(x, y, dims):
    xh, xl = split(x)
    yh, yl = split(y)
    return mm(xh, yh, dims) + mm(xh, yl, dims) + mm(xl, yh, dims)


def sigmoid(x):
    return 1.0 / (1.0 + jnp.exp(-x))


def turn(a, k, n):
    if n & (n - 1):
        return lax.rem(a + k, n)
    out, bit = 0, 1
    while bit < n:
        out = out + bit * lax.rem((a // bit) + (k // bit), 2)
        bit *= 2
    return out


def kernel(
    nsec, nview, factor,
    tok_hbm, gain_hbm, w_hbm, list_hbm, count_ref, cam_ref, want_hbm,
    image_ref, grad_ref, loss_ref,
    tok_ref, gain_ref, w_ref, list_ref, want_ref,
    perm, asked, wanted, found, given, lists, where, fits, norms, grads, dhead, mine, theirs,
    losses, loss_mine, loss_theirs,
    s_in, s_small, r_small, s_norm, r_norm, s_grad, r_grad, s_part, r_part, s_loss, r_loss,
):
    group = nsec * nview
    nlo = 2 if nview % 2 == 0 else 1
    nhi = nview // nlo
    sec, view, scene = lax.axis_index("section"), lax.axis_index("view"), lax.axis_index("scene")
    hi, lo = view // nlo, lax.rem(view, nlo)
    me = sec * nview + view
    tok_rows, width = tok_ref.shape
    outw = w_ref.shape[1]
    gpt = outw // PARAMS
    tiles, K = list_ref.shape
    slots = tiles * K
    tokens = group * tok_rows
    pix = SIDE * SIDE
    cap = 2 * slots // group
    per = 128 // cap
    packs = group // per
    ahead = where.shape[0] > 1

    def local(n, src, dst):
        return pltpu.make_async_copy(src, dst, s_in.at[n])

    loads = [
        local(0, list_hbm, list_ref),
        local(1, tok_hbm, tok_ref),
        local(2, gain_hbm, gain_ref),
        local(3, w_hbm, w_ref),
        local(4, want_hbm, want_ref),
    ]
    for load in loads:
        load.start()

    def peer(i):
        s = turn(sec, lax.rem(i, nsec), nsec)
        l = turn(lo, lax.rem(i // nsec, nlo), nlo)
        h = turn(hi, i // (nsec * nlo), nhi)
        v = h * nlo + l
        return s * nview + v, (s, v, scene)

    def place_of(s, l, h):
        return (s * nlo + l) * nhi + h

    partner = (sec, view, 1 - scene)
    barrier = pltpu.get_barrier_semaphore()

    @pl.loop(1, group)
    def _(i):
        pl.semaphore_signal(barrier, inc=1, device_id=peer(i)[1], device_id_type=MESH)

    pl.semaphore_signal(barrier, inc=1, device_id=partner, device_id_type=MESH)

    loads[0].wait()
    number = jnp.concatenate([list_ref[pl.ds(b, 1), :] for b in range(tiles)], axis=1)
    token = number // gpt
    gauss = number - token * gpt
    owner = token // tok_rows
    inner = token - owner * tok_rows
    ow_sec = owner // nview
    ow_hi = (owner - ow_sec * nview) // nlo
    ow_lo = owner - ow_sec * nview - ow_hi * nlo
    row = place_of(ow_sec, ow_lo, ow_hi) * tok_rows + inner
    for b in range(tiles):
        cut = slice(b * K, (b + 1) * K)
        lists[me, pl.ds(b, 1), :] = row[:, cut]
        lists[me, pl.ds(tiles + b, 1), :] = gauss[:, cut]
    mask = jnp.where(lax.broadcasted_iota(jnp.int32, (group, slots), 0) == owner, 1.0, 0.0)
    earlier = jnp.where(
        lax.broadcasted_iota(jnp.int32, (slots, slots), 0)
        < lax.broadcasted_iota(jnp.int32, (slots, slots), 1),
        1.0, 0.0,
    ).astype(BF16)
    rank = jnp.sum(mask * mm(mask.astype(BF16), earlier, NN), axis=0, keepdims=True)
    dest = owner * cap + rank.astype(jnp.int32)
    perm[...] = jnp.where(
        lax.broadcasted_iota(jnp.int32, (group * cap, slots), 0) == dest, 1.0, 0.0
    ).astype(BF16)
    asks = jnp.concatenate(
        [inner.astype(F32), gauss.astype(F32), jnp.zeros((6, slots), F32)], axis=0
    ).astype(BF16)
    requests = mm(asks, perm[...], NT)
    for i in range(packs):
        asked[i] = requests[:, i * 128 : (i + 1) * 128]
    wanted[me] = asked[me // per]

    pl.semaphore_wait(barrier, group)

    def small(n, src, dst, where_to):
        return pltpu.make_async_remote_copy(
            src_ref=src, dst_ref=dst, send_sem=s_small.at[n], recv_sem=r_small.at[n],
            device_id=where_to, device_id_type=MESH,
        )

    def all_small(n, buf):
        span = buf.at[pl.ds(0, group - 1)]
        return small(n, span, span, partner)

    @pl.loop(1, group)
    def _(i):
        j, to = peer(i)
        small(0, asked.at[j // per], wanted.at[me], to).start()

    @pl.loop(1, group)
    def _(i):
        small(1, lists.at[me], lists.at[me], peer(i)[1]).start()

    loads[1].wait()
    loads[2].wait()
    spot = place_of(sec, lo, hi)
    x = tok_ref[...].astype(F32)
    scale = lax.rsqrt(jnp.mean(x * x, axis=-1, keepdims=True) + 1e-06)
    normed = (x * scale * gain_ref[...]).astype(BF16)
    norms[spot] = normed

    def norm_copy(n, span, to):
        return pltpu.make_async_remote_copy(
            src_ref=norms.at[span], dst_ref=norms.at[span], send_sem=s_norm.at[n],
            recv_sem=r_norm.at[n], device_id=to, device_id_type=MESH,
        )

    def line_copy(k):
        h = turn(hi, k, nhi)
        return norm_copy(0, pl.ds(spot, 1), (sec, h * nlo + lo, scene))

    line = pl.ds((sec * nlo + lo) * nhi, nhi)
    beside = [(turn(sec, k, nsec), lo) for k in range(1, nsec)]
    below = [(sec, turn(lo, k, nlo)) for k in range(1, nlo)]

    @pl.loop(1, nhi)
    def _(k):
        line_copy(k).start()

    loads[3].wait()
    head = mm(normed, w_ref[...], NN)
    stack = jnp.concatenate(
        [head[:, p * gpt : (p + 1) * gpt] for p in range(PARAMS)], axis=0
    ).astype(BF16)
    er = lax.broadcasted_iota(jnp.int32, (PARAMS * tok_rows, PARAMS * tok_rows), 0)
    ec = lax.broadcasted_iota(jnp.int32, (PARAMS * tok_rows, PARAMS * tok_rows), 1)
    swap = jnp.where(ec == (er % PARAMS) * tok_rows + er // PARAMS, 1.0, 0.0).astype(BF16)
    table = mm(swap, stack, NN).astype(BF16)

    lane = lax.broadcasted_iota(jnp.int32, (8, 128), 1)
    mine_at = lax.rem(me, per)

    def gathered(buf):
        out = []
        for i in range(packs):
            total = None
            for k in range(per):
                q = lax.rem(mine_at + k, per)
                block = buf[i * per + q]
                if k:
                    block = pltpu.roll(block, k * cap, 1)
                total = block if total is None else jnp.where(lane // cap == q, block, total)
            out.append(total)
        return jnp.concatenate(out, axis=1)

    all_small(0, wanted).wait_recv()
    asks_in = gathered(wanted)
    ask_g = asks_in[1:2]
    ask_t = asks_in[0:1]
    hot = jnp.where(
        lax.broadcasted_iota(jnp.int32, (gpt, group * cap), 0) == ask_g.astype(jnp.int32), 1.0, 0.0
    ).astype(BF16)
    spread_rows = mm(table, hot, NN)
    answer = jnp.zeros((PARAMS, group * cap), F32)
    for t in range(tok_rows):
        answer = jnp.where(
            ask_t == float(t), spread_rows[t * PARAMS : (t + 1) * PARAMS], answer
        )
    for i in range(packs):
        found[i] = answer[:, i * 128 : (i + 1) * 128]
    given[me] = found[me // per]

    @pl.loop(1, group)
    def _(i):
        j, to = peer(i)
        small(2, found.at[j // per], given.at[me], to).start()

    norm_copy(0, pl.ds(0, nhi - 1), partner).wait_recv()
    for n, (s, l) in enumerate(beside + below):
        norm_copy(1 + n, line, (s, hi * nlo + l, scene)).start()

    all_small(1, lists).wait_recv()
    row_at = lax.broadcasted_iota(jnp.int32, (tokens, K), 0)
    gauss_at = lax.broadcasted_iota(jnp.int32, (gpt, K), 0)

    @pl.loop(0, group)
    def _(j):
        for b in range(tiles):
            cut = slice(b * K, (b + 1) * K)
            at = lists[j, pl.ds(b, 1), :]
            if ahead:
                where[j, :, cut] = jnp.where(row_at == at, 1.0, 0.0).astype(BF16)
            g = lists[j, pl.ds(tiles + b, 1), :]
            fits[j, :, cut] = jnp.where(gauss_at == g, 1.0, 0.0).astype(BF16)

    all_small(2, given).wait_recv()
    picked = mm(gathered(given).astype(BF16), perm[...], NN)
    rows = [picked[p : p + 1] for p in range(PARAMS)]
    loads[4].wait()

    place = lax.broadcasted_iota(jnp.int32, (1, pix), 1)
    across = ((place % SIDE).astype(F32) + 0.5) * (2.0 / SIDE) - 1.0
    down = ((place // SIDE).astype(F32) + 0.5) * (2.0 / SIDE) - 1.0
    ka = lax.broadcasted_iota(jnp.int32, (K, K), 0)
    kb = lax.broadcasted_iota(jnp.int32, (K, K), 1)
    lower = jnp.where(kb < ka, 1.0, 0.0).astype(BF16)
    upper = jnp.where(kb > ka, 1.0, 0.0).astype(BF16)
    ones = jnp.ones((8, pix), BF16)
    per_view = (tiles * group) // VIEWS
    slot = lax.broadcasted_iota(jnp.int32, (1, K), 1)
    loss_part = jnp.zeros((1, K), F32)
    outs = []

    for b in range(tiles):
        cut = slice(b * K, (b + 1) * K)
        mx, my, mz, ls, op, cr, cg, cb = [r[:, cut] for r in rows]
        vi = (me * tiles + b) // per_view
        cam = [cam_ref[vi, n] for n in range(8)]
        live = jnp.where(slot < count_ref[b], 1.0, 0.0)
        sx = jnp.tanh(cam[0] * mx + cam[1] * my + cam[2] * mz + cam[3])
        sy = jnp.tanh(cam[4] * mx + cam[5] * my + cam[6] * mz + cam[7])
        spread = jnp.exp(-2.0 * ls)
        sop = sigmoid(op)
        amp = 0.3 * sop * live
        shade = sigmoid(jnp.concatenate([cr, cg, cb], axis=0))
        shade8 = jnp.concatenate([shade, jnp.zeros((5, K), F32)], axis=0)
        cols = jnp.concatenate([sx, sy, spread, amp, jnp.zeros((K - 4, K), F32)], axis=0).T
        csx, csy, csp, camp = [cols[:, n : n + 1] for n in range(4)]
        dx = across - csx
        dy = down - csy
        r2 = dx * dx + dy * dy
        alpha = camp * jnp.exp(-0.5 * r2 * csp)
        rest = 1.0 - alpha
        trans = jnp.exp(mm2(lower, jnp.log(rest), NN))
        weight = alpha * trans
        colour = mm3(shade8, weight, NN)
        for c in range(3):
            image_ref[pl.ds(b, 1), c * pix : (c + 1) * pix] = colour[c : c + 1].astype(BF16)
        want = jnp.concatenate(
            [want_ref[pl.ds(b, 1), c * pix : (c + 1) * pix].astype(F32) for c in range(3)]
            + [jnp.zeros((5, pix), F32)],
            axis=0,
        )
        diff = colour - want
        sq = jnp.sum(diff * diff, axis=0, keepdims=True)
        part = sq[:, :K]
        for n in range(1, pix // K):
            part = part + sq[:, n * K : (n + 1) * K]
        loss_part = loss_part + part * factor
        dcol = (2.0 * factor) * diff
        dw = mm3(shade8, dcol, TN)
        dshade = mm3(dcol, weight, NT)
        dww = dw * weight
        dlogs = mm2(upper, dww, NN)
        h = dww - dlogs * alpha / rest
        s_h = mm2(ones, h, NT)[0:1]
        s_x = mm2(ones, h * dx, NT)[0:1]
        s_y = mm2(ones, h * dy, NT)[0:1]
        s_r = mm2(ones, h * r2, NT)[0:1]
        px = spread * s_x * (1.0 - sx * sx)
        py = spread * s_y * (1.0 - sy * sy)
        dcolour = dshade[0:3] * shade * (1.0 - shade)
        outs.append(
            jnp.concatenate(
                [
                    cam[0] * px + cam[4] * py,
                    cam[1] * px + cam[5] * py,
                    cam[2] * px + cam[6] * py,
                    spread * s_r,
                    (1.0 - sop) * s_h,
                    dcolour,
                ],
                axis=0,
            )
        )
    half = tiles // 2
    grads[me] = jnp.concatenate(
        [jnp.concatenate(outs[:half], axis=1), jnp.concatenate(outs[half:], axis=1)], axis=0
    ).astype(BF16)
    losses[me] = loss_part

    def push(n, buf, i, recv):
        j, to = peer(i)
        return pltpu.make_async_remote_copy(
            src_ref=buf.at[me], dst_ref=buf.at[me], send_sem=s_grad.at[n],
            recv_sem=recv, device_id=to, device_id_type=MESH,
        )

    @pl.loop(1, group)
    def _(i):
        push(0, grads, i, r_grad.at[me]).start()

    @pl.loop(1, group)
    def _(i):
        push(1, losses, i, s_loss.at[1]).start()

    nb = nsec - 1
    ns = nlo - 1
    for n in range(nb + ns):
        norm_copy(1 + n, line, partner).wait_recv()
    cut_rows = tok_rows // 2
    far = []
    for a, (s, _) in enumerate(beside):
        for b, (_, l) in enumerate(below):
            far.append((a, b, s, l))

    def far_copies():
        out = []
        base = 1 + nb + ns
        for m, (a, b, s, l) in enumerate(far):
            down_line = pl.ds((sec * nlo + l) * nhi, nhi)
            side_line = pl.ds((s * nlo + lo) * nhi, nhi)
            first = pl.ds(0, cut_rows)
            second = pl.ds(cut_rows, tok_rows - cut_rows)
            for n, span, part, to in (
                (base + 2 * m, down_line, first, (s, hi * nlo + lo, scene)),
                (base + 2 * m + 1, side_line, second, (sec, hi * nlo + l, scene)),
            ):
                out.append(
                    pltpu.make_async_remote_copy(
                        src_ref=norms.at[span, part], dst_ref=norms.at[span, part],
                        send_sem=s_norm.at[n], recv_sem=r_norm.at[n], device_id=to,
                        device_id_type=MESH,
                    )
                )
        return out

    for copy in far_copies():
        copy.start()

    @pl.loop(0, group)
    def _(i):
        j = peer(i)[0]

        @pl.when(i > 0)
        def _():
            push(0, grads, i, r_grad.at[j]).wait_recv()

        got = grads[j]
        fit = fits[j]
        wide = half * K
        spreadout = jnp.concatenate(
            [
                jnp.concatenate(
                    [
                        fit[:, :wide] * got[p : p + 1],
                        fit[:, wide:] * got[PARAMS + p : PARAMS + p + 1],
                    ],
                    axis=1,
                )
                for p in range(PARAMS)
            ],
            axis=0,
        )
        if not ahead:
            for b in range(tiles):
                at = lists[j, pl.ds(b, 1), :]
                where[0, :, b * K : (b + 1) * K] = jnp.where(row_at == at, 1.0, 0.0).astype(BF16)
        part = mm(where[j if ahead else 0], spreadout, NT)

        @pl.when(i == 0)
        def _():
            dhead[...] = part

        @pl.when(i > 0)
        def _():
            dhead[...] += part

    loss_all = losses.at[pl.ds(0, group - 1)]
    pltpu.make_async_remote_copy(
        src_ref=loss_all, dst_ref=loss_all, send_sem=s_grad.at[1], recv_sem=s_loss.at[1],
        device_id=partner, device_id_type=MESH,
    ).wait_recv()
    loss_mine[...] = jnp.broadcast_to(jnp.sum(losses[...], axis=0), loss_mine.shape)
    for copy in far_copies():
        copy.wait_recv()
    loss_copy = pltpu.make_async_remote_copy(
        src_ref=loss_mine, dst_ref=loss_theirs, send_sem=s_loss.at[0], recv_sem=r_loss,
        device_id=partner, device_id_type=MESH,
    )
    dh = dhead[...].astype(BF16)
    dhead_rows = 256
    chunks = width // dhead_rows

    def part_copy(n):
        span = pl.ds(n * dhead_rows, dhead_rows)
        return pltpu.make_async_remote_copy(
            src_ref=mine.at[span], dst_ref=theirs.at[span],
            send_sem=s_part.at[n], recv_sem=r_part.at[n],
            device_id=partner, device_id_type=MESH,
        )

    for n in range(chunks):
        a = norms[:, :, n * dhead_rows : (n + 1) * dhead_rows].reshape(tokens, dhead_rows)
        mine[n * dhead_rows : (n + 1) * dhead_rows, :] = mm(a, dh, TN).astype(BF16)
        if n == 0:
            loss_copy.start()
        else:
            part_copy(n - 1).start()
    part_copy(chunks - 1).start()

    for n in range(chunks):
        part_copy(n).wait_recv()
        span = slice(n * dhead_rows, (n + 1) * dhead_rows)
        grad_ref[span, :] = (mine[span, :].astype(F32) + theirs[span, :].astype(F32)).astype(BF16)
    loss_copy.wait_recv()
    loss_ref[...] = jnp.broadcast_to(
        jnp.sum(loss_mine[0:1] + loss_theirs[0:1], keepdims=True), loss_ref.shape
    )

    loss_copy.wait_send()
    for n in range(chunks):
        part_copy(n).wait_send()
    all_small(0, wanted).wait_send()
    all_small(1, lists).wait_send()
    all_small(2, given).wait_send()
    grad_all = grads.at[pl.ds(0, group - 1)]
    pltpu.make_async_remote_copy(
        src_ref=grad_all, dst_ref=grad_all, send_sem=s_grad.at[0], recv_sem=r_grad.at[0],
        device_id=partner, device_id_type=MESH,
    ).wait_send()
    pltpu.make_async_remote_copy(
        src_ref=loss_all, dst_ref=loss_all, send_sem=s_grad.at[1], recv_sem=s_loss.at[1],
        device_id=partner, device_id_type=MESH,
    ).wait_send()
    norm_copy(0, pl.ds(0, nhi - 1), partner).wait_send()
    for n in range(nb + ns):
        norm_copy(1 + n, line, partner).wait_send()
    for copy in far_copies():
        copy.wait_send()


def solution(mesh):
    nsec, nview, nscene = mesh.shape["section"], mesh.shape["view"], mesh.shape["scene"]
    group = nsec * nview
    nlo = 2 if nview % 2 == 0 else 1

    def body(tokens, norm_gain, head_weight, tile_lists, tile_counts, cameras, targets):
        tok_rows, width = tokens.shape[1:]
        outw = head_weight.shape[1]
        gpt = outw // PARAMS
        tiles, K = tile_lists.shape[1:]
        slots = tiles * K
        cap = 2 * slots // group
        packs = group * cap // 128
        factor = 1.0 / (nscene * tiles * group)
        ahead = group * group * tok_rows * slots <= 2**24
        flows = 1 + (nsec - 1) + (nlo - 1) + 2 * (nsec - 1) * (nlo - 1)
        vmem = pl.BlockSpec(memory_space=pltpu.VMEM)
        smem = pl.BlockSpec(memory_space=pltpu.SMEM)
        hbm = pl.BlockSpec(memory_space=pl.ANY)
        dma = pltpu.SemaphoreType.DMA
        image, grad, loss = pl.pallas_call(
            functools.partial(kernel, nsec, nview, factor),
            out_shape=(
                jax.ShapeDtypeStruct((tiles, targets.shape[2]), BF16),
                jax.ShapeDtypeStruct((width, outw), BF16),
                jax.ShapeDtypeStruct((8, 128), F32),
            ),
            in_specs=[hbm, hbm, hbm, hbm, smem, smem, hbm],
            out_specs=(vmem, vmem, vmem),
            scratch_shapes=[
                pltpu.VMEM((tok_rows, width), BF16),
                pltpu.VMEM((1, width), F32),
                pltpu.VMEM((width, outw), BF16),
                pltpu.VMEM((tiles, K), jnp.int32),
                pltpu.VMEM((tiles, targets.shape[2]), BF16),
                pltpu.VMEM((group * cap, slots), BF16),
                pltpu.VMEM((packs, 8, 128), F32),
                pltpu.VMEM((group, 8, 128), F32),
                pltpu.VMEM((packs, 8, 128), F32),
                pltpu.VMEM((group, 8, 128), F32),
                pltpu.VMEM((group, 2 * tiles, K), jnp.int32),
                pltpu.VMEM((group if ahead else 1, group * tok_rows, slots), BF16),
                pltpu.VMEM((group, gpt, slots), BF16),
                pltpu.VMEM((group, tok_rows, width), BF16),
                pltpu.VMEM((group, 2 * PARAMS, slots // 2), BF16),
                pltpu.VMEM((group * tok_rows, outw), F32),
                pltpu.VMEM((width, outw), BF16),
                pltpu.VMEM((width, outw), BF16),
                pltpu.VMEM((group, 1, K), F32),
                pltpu.VMEM((8, K), F32),
                pltpu.VMEM((8, K), F32),
                dma((5,)),
                dma((3,)), dma((3,)),
                dma((flows,)), dma((flows,)),
                dma((2,)), dma((group,)),
                dma((width // 256,)), dma((width // 256,)),
                dma((2,)), dma,
            ],
            compiler_params=pltpu.CompilerParams(
                collective_id=0, has_side_effects=True, vmem_limit_bytes=60 * 1024 * 1024
            ),
        )(
            tokens[0], norm_gain[None], head_weight, tile_lists[0], tile_counts[0], cameras[0],
            targets[0],
        )
        return image[None], grad.astype(F32), loss[0, 0]

    in_specs = (
        P("scene", ("section", "view"), None),
        P(),
        P(),
        P("scene", ("section", "view"), None),
        P("scene", ("section", "view")),
        P("scene", None, None),
        P("scene", ("section", "view"), None),
    )
    out_specs = (P("scene", ("section", "view"), None), P(), P())
    return jax.shard_map(body, mesh=mesh, in_specs=in_specs, out_specs=out_specs, check_vma=False)
```

time: 57.9 us -> 45.2 us (0.78)
  the two profiles are of different devices: /device:TPU:27 before, /device:TPU:1 now
where the time goes in v1:
time: 45.2 us; the launch traced here: 45 us
  Pallas kernels  39.7 us (88%)
  other arithmetic  2.83 us (6%)
  local copies, waits for them, and re-layouts  1.79 us (4%)
  between operations  0.65 us (1%)
    pallas_call x1, Pallas kernels, body(): pl.pallas_call(functools.partial(kernel, nsec, nview, factor), out_shape=...  39.7 us
    convert_element_type x1, other arithmetic, body(): return (image[None], grad.astype(F32), loss[0, 0])  2.83 us
    slice x1, local copies, waits for them, and re-layouts, body(): return (image[None], grad.astype(F32), loss[0, 0])  1.2 us

profile of v1, /device:TPU:1, one launch (start us, length us, event | category | flops | bytes accessed | tf_op | source)
XLA Modules:
  0.0 45.0 jit_solution(17175357658080328607)
XLA Ops:
  0.6 39.7 %shard_map.94 = (bf16[4,768]{1,0:T(4,128)(2,1)}, bf16[1024,512]{1,0:T(8,128)(2,1)}, f32[8,128]{1,0:T(8,128)}) custom-call(bf16[32,1024]{1,0:T(8,128)(2,1)} %bitcast.8, f32[1,1024]{1,0:T(1,128)} %bitcast.11, bf16[1024,512]{1,0:T(8,128)(2,1)} %w_hbm.1, s32[4,128]{1,0:T(4,128)} %bitcast.12, s32[4]{0:T(128)} %bitcast.14, f32[2,8]{1,0:T(2,128)} %bitcast.13, ...), custom_call_target="tpu_custom_call" | custom-call | tf_op jit(solution)/shard_map/pallas_call | solution.py:518
  40.4 0.0 copy-start
  40.4 1.2 %slice.3 = f32[1,1]{1,0:T(1,128)} slice(f32[8,128]{1,0:T(8,128)} %get-tuple-element.8), slice={[0:1], [0:1]} | slice | bytes 8 | tf_op jit(solution)/shard_map/slice | solution.py:563
  41.6 2.8 %convert_element_type.3 = f32[1024,512]{1,0:T(8,128)} convert(bf16[1024,512]{1,0:T(8,128)(2,1)} %get-tuple-element.7) | non-fusion elementwise | flops 524288 | bytes 3145728 | tf_op jit(solution)/shard_map/convert_element_type | solution.py:563
  44.4 0.0 copy-done
  44.4 0.6 %copy.11 = bf16[1,4,768]{2,1,0:T(4,128)(2,1)} copy(bf16[1,4,768]{2,1,0:T(4,128)(2,1)S(1)} %bitcast.10) | data formatting | bytes 12288
Async XLA Ops:
  40.4 4.0 %copy-start = (bf16[4,768]{1,0:T(4,128)(2,1)S(1)}, bf16[4,768]{1,0:T(4,128)(2,1)}, u32[]{:S(2)}) copy-start(bf16[4,768]{1,0:T(4,128)(2,1)} %get-tuple-element.6) | copy-start | bytes 18436

commit v2 on v1

--- a/solution.py
+++ b/solution.py
@@ -9,10 +9,12 @@
 
 PARAMS = 8
 SIDE = 16
+BATCH = 4
 VIEWS = 2
 MESH = pl.DeviceIdType.MESH
 F32 = jnp.float32
 BF16 = jnp.bfloat16
+LOG2E = 1.4426950408889634
 NN = (((1,), (0,)), ((), ()))
 NT = (((1,), (1,)), ((), ()))
 TN = (((0,), (0,)), ((), ()))
@@ -26,17 +28,6 @@
     hi = x.astype(BF16)
     lo = (x - hi.astype(F32)).astype(BF16)
     return hi, lo
-
-
-def mm2(a, x, dims):
-    hi, lo = split(x)
-    return mm(a, hi, dims) + mm(a, lo, dims)
-
-
-def mm3(x, y, dims):
-    xh, xl = split(x)
-    yh, yl = split(y)
-    return mm(xh, yh, dims) + mm(xh, yl, dims) + mm(xl, yh, dims)
 
 
 def sigmoid(x):
@@ -58,7 +49,7 @@
     tok_hbm, gain_hbm, w_hbm, list_hbm, count_ref, cam_ref, want_hbm,
     image_ref, grad_ref, loss_ref,
     tok_ref, gain_ref, w_ref, list_ref, want_ref,
-    perm, asked, wanted, found, given, lists, where, fits, norms, grads, dhead, mine, theirs,
+    perm, asked, wanted, found, given, lists, where, fits, norms, grads, dhead, turned, mine, theirs,
     losses, loss_mine, loss_theirs,
     s_in, s_small, r_small, s_norm, r_norm, s_grad, r_grad, s_part, r_part, s_loss, r_loss,
 ):
@@ -79,6 +70,7 @@
     per = 128 // cap
     packs = group // per
     ahead = where.shape[0] > 1
+    batch = where.shape[2] // slots
 
     def local(n, src, dst):
         return pltpu.make_async_copy(src, dst, s_in.at[n])
@@ -243,20 +235,35 @@
     norm_copy(0, pl.ds(0, nhi - 1), partner).wait_recv()
     for n, (s, l) in enumerate(beside + below):
         norm_copy(1 + n, line, (s, hi * nlo + l, scene)).start()
+    stretch = nhi * tok_rows
+
+    def turn_line(n):
+        block = norms[n * nhi : (n + 1) * nhi].reshape(stretch, width)
+        turned[:, n * stretch : (n + 1) * stretch] = block.T
 
     all_small(1, lists).wait_recv()
     row_at = lax.broadcasted_iota(jnp.int32, (tokens, K), 0)
     gauss_at = lax.broadcasted_iota(jnp.int32, (gpt, K), 0)
 
+    def mark_rows(g, n):
+        for q in range(batch):
+            j = peer(g * batch + q)[0]
+            for b in range(tiles):
+                at = lists[j, pl.ds(b, 1), :]
+                where[n, :, (q * tiles + b) * K : (q * tiles + b + 1) * K] = jnp.where(
+                    row_at == at, 1.0, 0.0
+                ).astype(BF16)
+
+    @pl.loop(0, group // batch)
+    def _(g):
+        if ahead:
+            mark_rows(g, g)
+
     @pl.loop(0, group)
     def _(j):
         for b in range(tiles):
-            cut = slice(b * K, (b + 1) * K)
-            at = lists[j, pl.ds(b, 1), :]
-            if ahead:
-                where[j, :, cut] = jnp.where(row_at == at, 1.0, 0.0).astype(BF16)
-            g = lists[j, pl.ds(tiles + b, 1), :]
-            fits[j, :, cut] = jnp.where(gauss_at == g, 1.0, 0.0).astype(BF16)
+            at = lists[j, pl.ds(tiles + b, 1), :]
+            fits[j, :, b * K : (b + 1) * K] = jnp.where(gauss_at == at, 1.0, 0.0).astype(BF16)
 
     all_small(2, given).wait_recv()
     picked = mm(gathered(given).astype(BF16), perm[...], NN)
@@ -266,83 +273,97 @@
     place = lax.broadcasted_iota(jnp.int32, (1, pix), 1)
     across = ((place % SIDE).astype(F32) + 0.5) * (2.0 / SIDE) - 1.0
     down = ((place // SIDE).astype(F32) + 0.5) * (2.0 / SIDE) - 1.0
-    ka = lax.broadcasted_iota(jnp.int32, (K, K), 0)
-    kb = lax.broadcasted_iota(jnp.int32, (K, K), 1)
+    ka = lax.broadcasted_iota(jnp.int32, (K, 2 * K), 0)
+    kb = lax.rem(lax.broadcasted_iota(jnp.int32, (K, 2 * K), 1), K)
     lower = jnp.where(kb < ka, 1.0, 0.0).astype(BF16)
     upper = jnp.where(kb > ka, 1.0, 0.0).astype(BF16)
-    ones = jnp.ones((8, pix), BF16)
-    per_view = (tiles * group) // VIEWS
+    moments = jnp.concatenate(
+        [jnp.ones((1, pix), F32), across, down, across * across + down * down, jnp.zeros((4, pix), F32)],
+        axis=0,
+    ).astype(BF16)
+    vi = me * VIEWS // group
+    cam = [cam_ref[vi, n] for n in range(8)]
     slot = lax.broadcasted_iota(jnp.int32, (1, K), 1)
-    loss_part = jnp.zeros((1, K), F32)
-    outs = []
-
-    for b in range(tiles):
-        cut = slice(b * K, (b + 1) * K)
-        mx, my, mz, ls, op, cr, cg, cb = [r[:, cut] for r in rows]
-        vi = (me * tiles + b) // per_view
-        cam = [cam_ref[vi, n] for n in range(8)]
-        live = jnp.where(slot < count_ref[b], 1.0, 0.0)
-        sx = jnp.tanh(cam[0] * mx + cam[1] * my + cam[2] * mz + cam[3])
-        sy = jnp.tanh(cam[4] * mx + cam[5] * my + cam[6] * mz + cam[7])
-        spread = jnp.exp(-2.0 * ls)
-        sop = sigmoid(op)
-        amp = 0.3 * sop * live
-        shade = sigmoid(jnp.concatenate([cr, cg, cb], axis=0))
-        shade8 = jnp.concatenate([shade, jnp.zeros((5, K), F32)], axis=0)
-        cols = jnp.concatenate([sx, sy, spread, amp, jnp.zeros((K - 4, K), F32)], axis=0).T
-        csx, csy, csp, camp = [cols[:, n : n + 1] for n in range(4)]
+    live = jnp.concatenate(
+        [jnp.where(slot < count_ref[b], 1.0, 0.0) for b in range(tiles)], axis=1
+    )
+    mx, my, mz, ls, op = rows[:5]
+    sx = jnp.tanh(cam[0] * mx + cam[1] * my + cam[2] * mz + cam[3])
+    sy = jnp.tanh(cam[4] * mx + cam[5] * my + cam[6] * mz + cam[7])
+    spread = jnp.exp(-2.0 * ls)
+    sop = sigmoid(op)
+    amp = 0.3 * sop * live
+    shade = sigmoid(picked[5:8])
+    shade8 = jnp.concatenate([shade, jnp.zeros((5, slots), F32)], axis=0)
+    steep = (-0.5 * LOG2E) * jnp.minimum(spread, 1e38)
+    cols = jnp.concatenate([sx, sy, steep, amp, jnp.zeros((4, slots), F32)], axis=0).T
+    cuts = [slice(b * K, (b + 1) * K) for b in range(tiles)]
+
+    alphas, inverses, logs = [], [], []
+    for cut in cuts:
+        csx, csy, csp, camp = [cols[cut, n : n + 1] for n in range(4)]
         dx = across - csx
         dy = down - csy
-        r2 = dx * dx + dy * dy
-        alpha = camp * jnp.exp(-0.5 * r2 * csp)
+        alpha = camp * jnp.exp2((dx * dx + dy * dy) * csp)
         rest = 1.0 - alpha
-        trans = jnp.exp(mm2(lower, jnp.log(rest), NN))
-        weight = alpha * trans
-        colour = mm3(shade8, weight, NN)
-        for c in range(3):
-            image_ref[pl.ds(b, 1), c * pix : (c + 1) * pix] = colour[c : c + 1].astype(BF16)
+        alphas.append(alpha)
+        inverses.append(alpha / rest)
+        logs.append(jnp.concatenate(split(jnp.log(rest)), axis=0))
+    befores = [mm(lower, x, NN) for x in logs]
+    weights = [alpha * jnp.exp(before) for alpha, before in zip(alphas, befores)]
+    packed = [weight.astype(BF16) for weight in weights]
+    shade_hi, shade_lo = split(shade8)
+    shade_two = jnp.concatenate([shade_hi, shade_lo], axis=0)
+    colours = []
+    for cut, weight in zip(cuts, packed):
+        both = mm(shade_two[:, cut], weight, NN)
+        colours.append(both[:8] + both[8:])
+    loss_part = jnp.zeros((1, K), F32)
+    dcols = []
+    for b in range(tiles):
         want = jnp.concatenate(
             [want_ref[pl.ds(b, 1), c * pix : (c + 1) * pix].astype(F32) for c in range(3)]
             + [jnp.zeros((5, pix), F32)],
             axis=0,
         )
-        diff = colour - want
+        for c in range(3):
+            image_ref[pl.ds(b, 1), c * pix : (c + 1) * pix] = colours[b][c : c + 1].astype(BF16)
+        diff = colours[b] - want
         sq = jnp.sum(diff * diff, axis=0, keepdims=True)
-        part = sq[:, :K]
-        for n in range(1, pix // K):
-            part = part + sq[:, n * K : (n + 1) * K]
-        loss_part = loss_part + part * factor
-        dcol = (2.0 * factor) * diff
-        dw = mm3(shade8, dcol, TN)
-        dshade = mm3(dcol, weight, NT)
-        dww = dw * weight
-        dlogs = mm2(upper, dww, NN)
-        h = dww - dlogs * alpha / rest
-        s_h = mm2(ones, h, NT)[0:1]
-        s_x = mm2(ones, h * dx, NT)[0:1]
-        s_y = mm2(ones, h * dy, NT)[0:1]
-        s_r = mm2(ones, h * r2, NT)[0:1]
-        px = spread * s_x * (1.0 - sx * sx)
-        py = spread * s_y * (1.0 - sy * sy)
-        dcolour = dshade[0:3] * shade * (1.0 - shade)
-        outs.append(
-            jnp.concatenate(
-                [
-                    cam[0] * px + cam[4] * py,
-                    cam[1] * px + cam[5] * py,
-                    cam[2] * px + cam[6] * py,
-                    spread * s_r,
-                    (1.0 - sop) * s_h,
-                    dcolour,
-                ],
-                axis=0,
-            )
-        )
-    half = tiles // 2
-    grads[me] = jnp.concatenate(
-        [jnp.concatenate(outs[:half], axis=1), jnp.concatenate(outs[half:], axis=1)], axis=0
-    ).astype(BF16)
-    losses[me] = loss_part
+        for n in range(0, pix, K):
+            loss_part = loss_part + sq[:, n : n + K]
+        dcols.append(((2.0 * factor) * diff).astype(BF16))
+    losses[me] = loss_part * factor
+    dshade = jnp.concatenate([mm(d, w, NT) for d, w in zip(dcols, packed)], axis=1)
+    dwws = [
+        mm(shade_hi[:, cut], d, TN) * weight for cut, d, weight in zip(cuts, dcols, weights)
+    ]
+    dlogs = [mm(upper[:, :K], x.astype(BF16), NN) for x in dwws]
+    sums = []
+    for x, y, inverse in zip(dwws, dlogs, inverses):
+        h = x - y * inverse
+        both = mm(moments, jnp.concatenate(split(h), axis=0), NT)
+        sums.append(both[:, :K] + both[:, K:])
+    sums = jnp.concatenate(sums, axis=1)
+    s_h, s_u, s_v, s_q = [sums[n : n + 1] for n in range(4)]
+    s_x = s_u - sx * s_h
+    s_y = s_v - sy * s_h
+    s_r = s_q - 2.0 * (sx * s_u + sy * s_v) + (sx * sx + sy * sy) * s_h
+    px = spread * s_x * (1.0 - sx * sx)
+    py = spread * s_y * (1.0 - sy * sy)
+    out = jnp.concatenate(
+        [
+            cam[0] * px + cam[4] * py,
+            cam[1] * px + cam[5] * py,
+            cam[2] * px + cam[6] * py,
+            spread * s_r,
+            (1.0 - sop) * s_h,
+            dshade[0:3] * shade * (1.0 - shade),
+        ],
+        axis=0,
+    )
+    wide = slots // 2
+    grads[me] = jnp.concatenate([out[:, :wide], out[:, wide:]], axis=0).astype(BF16)
 
     def push(n, buf, i, recv):
         j, to = peer(i)
@@ -393,43 +414,46 @@
     for copy in far_copies():
         copy.start()
 
-    @pl.loop(0, group)
-    def _(i):
-        j = peer(i)[0]
-
-        @pl.when(i > 0)
-        def _():
-            push(0, grads, i, r_grad.at[j]).wait_recv()
-
-        got = grads[j]
-        fit = fits[j]
-        wide = half * K
-        spreadout = jnp.concatenate(
-            [
+    def gather_batch(g, n):
+        sides = []
+        for q in range(batch):
+            i = g * batch + q
+            j = peer(i)[0]
+            if isinstance(i, int):
+                if i > 0:
+                    push(0, grads, i, r_grad.at[j]).wait_recv()
+            else:
+                pl.when(i > 0)(lambda: push(0, grads, i, r_grad.at[j]).wait_recv())
+            got = grads[j]
+            fit = fits[j]
+            sides.append(
                 jnp.concatenate(
                     [
-                        fit[:, :wide] * got[p : p + 1],
-                        fit[:, wide:] * got[PARAMS + p : PARAMS + p + 1],
+                        jnp.concatenate(
+                            [
+                                fit[:, :wide] * got[p : p + 1],
+                                fit[:, wide:] * got[PARAMS + p : PARAMS + p + 1],
+                            ],
+                            axis=1,
+                        )
+                        for p in range(PARAMS)
                     ],
-                    axis=1,
+                    axis=0,
                 )
-                for p in range(PARAMS)
-            ],
-            axis=0,
-        )
-        if not ahead:
-            for b in range(tiles):
-                at = lists[j, pl.ds(b, 1), :]
-                where[0, :, b * K : (b + 1) * K] = jnp.where(row_at == at, 1.0, 0.0).astype(BF16)
-        part = mm(where[j if ahead else 0], spreadout, NT)
-
-        @pl.when(i == 0)
-        def _():
-            dhead[...] = part
-
-        @pl.when(i > 0)
-        def _():
-            dhead[...] += part
+            )
+        return mm(jnp.concatenate(sides, axis=1), where[n], NT)
+
+    if ahead:
+        dhead[...] = gather_batch(0, 0)
+        for g in range(1, group // batch):
+            dhead[...] += gather_batch(g, g)
+    else:
+        dhead[...] = jnp.zeros_like(dhead)
+
+        @pl.loop(0, group // batch)
+        def _(g):
+            mark_rows(g, 0)
+            dhead[...] += gather_batch(g, 0)
 
     loss_all = losses.at[pl.ds(0, group - 1)]
     pltpu.make_async_remote_copy(
@@ -443,6 +467,8 @@
         src_ref=loss_mine, dst_ref=loss_theirs, send_sem=s_loss.at[0], recv_sem=r_loss,
         device_id=partner, device_id_type=MESH,
     )
+    for n in range(nsec * nlo):
+        turn_line(n)
     dh = dhead[...].astype(BF16)
     dhead_rows = 256
     chunks = width // dhead_rows
@@ -456,8 +482,8 @@
         )
 
     for n in range(chunks):
-        a = norms[:, :, n * dhead_rows : (n + 1) * dhead_rows].reshape(tokens, dhead_rows)
-        mine[n * dhead_rows : (n + 1) * dhead_rows, :] = mm(a, dh, TN).astype(BF16)
+        span = slice(n * dhead_rows, (n + 1) * dhead_rows)
+        mine[span, :] = mm(turned[span, :], dh, NT).astype(BF16)
         if n == 0:
             loss_copy.start()
         else:
@@ -510,6 +536,7 @@
         packs = group * cap // 128
         factor = 1.0 / (nscene * tiles * group)
         ahead = group * group * tok_rows * slots <= 2**24
+        batch = min(BATCH, group)
         flows = 1 + (nsec - 1) + (nlo - 1) + 2 * (nsec - 1) * (nlo - 1)
         vmem = pl.BlockSpec(memory_space=pltpu.VMEM)
         smem = pl.BlockSpec(memory_space=pltpu.SMEM)
@@ -536,11 +563,12 @@
                 pltpu.VMEM((packs, 8, 128), F32),
                 pltpu.VMEM((group, 8, 128), F32),
                 pltpu.VMEM((group, 2 * tiles, K), jnp.int32),
-                pltpu.VMEM((group if ahead else 1, group * tok_rows, slots), BF16),
+                pltpu.VMEM((group // batch if ahead else 1, group * tok_rows, batch * slots), BF16),
                 pltpu.VMEM((group, gpt, slots), BF16),
                 pltpu.VMEM((group, tok_rows, width), BF16),
                 pltpu.VMEM((group, 2 * PARAMS, slots // 2), BF16),
-                pltpu.VMEM((group * tok_rows, outw), F32),
+                pltpu.VMEM((outw, group * tok_rows), F32),
+                pltpu.VMEM((width, group * tok_rows), BF16),
                 pltpu.VMEM((width, outw), BF16),
                 pltpu.VMEM((width, outw), BF16),
                 pltpu.VMEM((group, 1, K), F32),

time: 45.2 us -> 40.1 us (0.89)
  Pallas kernels: 39.7 us -> 34.6 us
    pallas_call x1, Pallas kernels: 39.7 us -> 34.6 us  [body(): pl.pallas_call(functools.partial(kernel, nsec, nview, factor), out_shape=...]
where the time goes in v2:
time: 40.1 us; the launch traced here: 39.9 us
  Pallas kernels  34.6 us (86%)
  other arithmetic  2.83 us (7%)
  local copies, waits for them, and re-layouts  1.79 us (4%)
  between operations  0.65 us (2%)
    pallas_call x1, Pallas kernels, body(): pl.pallas_call(functools.partial(kernel, nsec, nview, factor), out_shape=...  34.6 us
    convert_element_type x1, other arithmetic, body(): return (image[None], grad.astype(F32), loss[0, 0])  2.83 us
    slice x1, local copies, waits for them, and re-layouts, body(): return (image[None], grad.astype(F32), loss[0, 0])  1.2 us

profile of v2, /device:TPU:1, one launch (start us, length us, event | category | flops | bytes accessed | tf_op | source)
XLA Modules:
  0.0 39.9 jit_solution(181967683734446722)
XLA Ops:
  0.6 34.6 %shard_map.94 = (bf16[4,768]{1,0:T(4,128)(2,1)}, bf16[1024,512]{1,0:T(8,128)(2,1)}, f32[8,128]{1,0:T(8,128)}) custom-call(bf16[32,1024]{1,0:T(8,128)(2,1)} %bitcast.8, f32[1,1024]{1,0:T(1,128)} %bitcast.11, bf16[1024,512]{1,0:T(8,128)(2,1)} %w_hbm.1, s32[4,128]{1,0:T(4,128)} %bitcast.12, s32[4]{0:T(128)} %bitcast.14, f32[2,8]{1,0:T(2,128)} %bitcast.13, ...), custom_call_target="tpu_custom_call" | custom-call | tf_op jit(solution)/shard_map/pallas_call | solution.py:545
  35.2 0.0 copy-start
  35.2 1.2 %slice.3 = f32[1,1]{1,0:T(1,128)} slice(f32[8,128]{1,0:T(8,128)} %get-tuple-element.8), slice={[0:1], [0:1]} | slice | bytes 8 | tf_op jit(solution)/shard_map/slice | solution.py:591
  36.4 2.8 %convert_element_type.3 = f32[1024,512]{1,0:T(8,128)} convert(bf16[1024,512]{1,0:T(8,128)(2,1)} %get-tuple-element.7) | non-fusion elementwise | flops 524288 | bytes 3145728 | tf_op jit(solution)/shard_map/convert_element_type | solution.py:591
  39.3 0.0 copy-done
  39.3 0.6 %copy.11 = bf16[1,4,768]{2,1,0:T(4,128)(2,1)} copy(bf16[1,4,768]{2,1,0:T(4,128)(2,1)S(1)} %bitcast.10) | data formatting | bytes 12288
Async XLA Ops:
  35.2 4.0 %copy-start = (bf16[4,768]{1,0:T(4,128)(2,1)S(1)}, bf16[4,768]{1,0:T(4,128)(2,1)}, u32[]{:S(2)}) copy-start(bf16[4,768]{1,0:T(4,128)(2,1)} %get-tuple-element.6) | copy-start | bytes 18436

commit v3 on v2

--- a/solution.py
+++ b/solution.py
@@ -9,7 +9,9 @@
 
 PARAMS = 8
 SIDE = 16
-BATCH = 4
+BATCH = 2
+STORES = 1
+LATE = 1
 VIEWS = 2
 MESH = pl.DeviceIdType.MESH
 F32 = jnp.float32
@@ -37,6 +39,13 @@
 def turn(a, k, n):
     if n & (n - 1):
         return lax.rem(a + k, n)
+    if isinstance(k, int):
+        bit = 1
+        while bit < n:
+            if k & bit:
+                a = a + bit - 2 * bit * lax.rem(a // bit, 2)
+            bit *= 2
+        return a
     out, bit = 0, 1
     while bit < n:
         out = out + bit * lax.rem((a // bit) + (k // bit), 2)
@@ -54,7 +63,7 @@
     s_in, s_small, r_small, s_norm, r_norm, s_grad, r_grad, s_part, r_part, s_loss, r_loss,
 ):
     group = nsec * nview
-    nlo = 2 if nview % 2 == 0 else 1
+    nlo = 2
     nhi = nview // nlo
     sec, view, scene = lax.axis_index("section"), lax.axis_index("view"), lax.axis_index("scene")
     hi, lo = view // nlo, lax.rem(view, nlo)
@@ -85,9 +94,25 @@
     for load in loads:
         load.start()
 
+    known = {}
+
+    def each_peer(act):
+        if group <= 16:
+            for i in range(group - 1, 0, -1):
+                act(i)
+        else:
+            pl.loop(1, group)(act)
+
     def peer(i):
-        s = turn(sec, lax.rem(i, nsec), nsec)
-        l = turn(lo, lax.rem(i // nsec, nlo), nlo)
+        if isinstance(i, int):
+            if i not in known:
+                known[i] = find(i)
+            return known[i]
+        return find(i)
+
+    def find(i):
+        s = turn(sec, i % nsec, nsec)
+        l = turn(lo, (i // nsec) % nlo, nlo)
         h = turn(hi, i // (nsec * nlo), nhi)
         v = h * nlo + l
         return s * nview + v, (s, v, scene)
@@ -98,7 +123,7 @@
     partner = (sec, view, 1 - scene)
     barrier = pltpu.get_barrier_semaphore()
 
-    @pl.loop(1, group)
+    @each_peer
     def _(i):
         pl.semaphore_signal(barrier, inc=1, device_id=peer(i)[1], device_id_type=MESH)
 
@@ -114,10 +139,9 @@
     ow_hi = (owner - ow_sec * nview) // nlo
     ow_lo = owner - ow_sec * nview - ow_hi * nlo
     row = place_of(ow_sec, ow_lo, ow_hi) * tok_rows + inner
+    code = row * gpt + gauss
     for b in range(tiles):
-        cut = slice(b * K, (b + 1) * K)
-        lists[me, pl.ds(b, 1), :] = row[:, cut]
-        lists[me, pl.ds(tiles + b, 1), :] = gauss[:, cut]
+        lists[me, pl.ds(b, 1), :] = code[:, b * K : (b + 1) * K]
     mask = jnp.where(lax.broadcasted_iota(jnp.int32, (group, slots), 0) == owner, 1.0, 0.0)
     earlier = jnp.where(
         lax.broadcasted_iota(jnp.int32, (slots, slots), 0)
@@ -133,6 +157,7 @@
         [inner.astype(F32), gauss.astype(F32), jnp.zeros((6, slots), F32)], axis=0
     ).astype(BF16)
     requests = mm(asks, perm[...], NT)
+    requests = requests[0:1] * float(gpt) + requests[1:2]
     for i in range(packs):
         asked[i] = requests[:, i * 128 : (i + 1) * 128]
     wanted[me] = asked[me // per]
@@ -149,12 +174,12 @@
         span = buf.at[pl.ds(0, group - 1)]
         return small(n, span, span, partner)
 
-    @pl.loop(1, group)
+    @each_peer
     def _(i):
         j, to = peer(i)
         small(0, asked.at[j // per], wanted.at[me], to).start()
 
-    @pl.loop(1, group)
+    @each_peer
     def _(i):
         small(1, lists.at[me], lists.at[me], peer(i)[1]).start()
 
@@ -166,23 +191,49 @@
     normed = (x * scale * gain_ref[...]).astype(BF16)
     norms[spot] = normed
 
-    def norm_copy(n, span, to):
+    def block(s, l, k):
+        return place_of(s, l, turn(hi, k, nhi))
+
+    half = tok_rows // 2
+    parts = {"whole": pl.ds(0, tok_rows), "top": pl.ds(0, half), "bottom": pl.ds(half, half)}
+    classes = [[0], [1], list(range(2, nhi))]
+    beside = (1 - sec, view, scene)
+    below = (sec, hi * nlo + 1 - lo, scene)
+
+    def norm_copy(n, ref, to):
         return pltpu.make_async_remote_copy(
-            src_ref=norms.at[span], dst_ref=norms.at[span], send_sem=s_norm.at[n],
-            recv_sem=r_norm.at[n], device_id=to, device_id_type=MESH,
+            src_ref=ref, dst_ref=ref, send_sem=s_norm.at[n], recv_sem=r_norm.at[n],
+            device_id=to, device_id_type=MESH,
         )
 
-    def line_copy(k):
-        h = turn(hi, k, nhi)
-        return norm_copy(0, pl.ds(spot, 1), (sec, h * nlo + lo, scene))
-
-    line = pl.ds((sec * nlo + lo) * nhi, nhi)
-    beside = [(turn(sec, k, nsec), lo) for k in range(1, nsec)]
-    below = [(sec, turn(lo, k, nlo)) for k in range(1, nlo)]
-
-    @pl.loop(1, nhi)
-    def _(k):
-        line_copy(k).start()
+    flows = {
+        "x": (3, beside, sec, lo, "whole"),
+        "y": (6, below, sec, lo, "whole"),
+        "far_x": (9, beside, sec, 1 - lo, "top"),
+        "far_y": (12, below, 1 - sec, lo, "bottom"),
+    }
+
+    def line_send(c):
+        for k in classes[c]:
+            to = (sec, turn(hi, k, nhi) * nlo + lo, scene)
+            norm_copy(c, norms.at[block(sec, lo, 0)], to).start()
+
+    def flow_send(name, c):
+        n, to, s, l, part = flows[name]
+        for k in classes[c]:
+            norm_copy(n + c, norms.at[block(s, l, k), parts[part]], to).start()
+
+    def flow_all(name, c):
+        n, _, _, _, part = flows[name]
+        return norm_copy(n + c, norms.at[pl.ds(0, len(classes[c])), parts[part]], partner)
+
+    def line_all(c):
+        return norm_copy(c, norms.at[pl.ds(0, len(classes[c]))], partner)
+
+    line_send(1)
+    flow_send("x", 0)
+    flow_send("y", 0)
+    line_send(2)
 
     loads[3].wait()
     head = mm(normed, w_ref[...], NN)
@@ -203,44 +254,49 @@
             total = None
             for k in range(per):
                 q = lax.rem(mine_at + k, per)
-                block = buf[i * per + q]
+                block = buf[i * per + q].astype(F32)
                 if k:
                     block = pltpu.roll(block, k * cap, 1)
-                total = block if total is None else jnp.where(lane // cap == q, block, total)
+                total = block if total is None else jnp.where(lane[: block.shape[0]] // cap == q, block, total)
             out.append(total)
         return jnp.concatenate(out, axis=1)
 
     all_small(0, wanted).wait_recv()
     asks_in = gathered(wanted)
-    ask_g = asks_in[1:2]
-    ask_t = asks_in[0:1]
+    ask = asks_in.astype(jnp.int32)
+    ask_t = ask // gpt
+    ask_g = ask - ask_t * gpt
     hot = jnp.where(
-        lax.broadcasted_iota(jnp.int32, (gpt, group * cap), 0) == ask_g.astype(jnp.int32), 1.0, 0.0
+        lax.broadcasted_iota(jnp.int32, (gpt, group * cap), 0) == ask_g, 1.0, 0.0
     ).astype(BF16)
     spread_rows = mm(table, hot, NN)
     answer = jnp.zeros((PARAMS, group * cap), F32)
     for t in range(tok_rows):
         answer = jnp.where(
-            ask_t == float(t), spread_rows[t * PARAMS : (t + 1) * PARAMS], answer
+            ask_t == t, spread_rows[t * PARAMS : (t + 1) * PARAMS], answer
         )
     for i in range(packs):
-        found[i] = answer[:, i * 128 : (i + 1) * 128]
+        found[i] = answer[:, i * 128 : (i + 1) * 128].astype(BF16)
     given[me] = found[me // per]
 
-    @pl.loop(1, group)
+    @each_peer
     def _(i):
         j, to = peer(i)
         small(2, found.at[j // per], given.at[me], to).start()
 
-    norm_copy(0, pl.ds(0, nhi - 1), partner).wait_recv()
-    for n, (s, l) in enumerate(beside + below):
-        norm_copy(1 + n, line, (s, hi * nlo + l, scene)).start()
     stretch = nhi * tok_rows
 
-    def turn_line(n):
-        block = norms[n * nhi : (n + 1) * nhi].reshape(stretch, width)
-        turned[:, n * stretch : (n + 1) * stretch] = block.T
-
+    def turn_line(s, l):
+        n = s * nlo + l
+        turned[n] = norms[pl.ds(n * nhi, nhi)].reshape(stretch, width).T
+
+    line_all(1).wait_recv()
+    flow_send("x", 1)
+    flow_send("y", 1)
+    flow_all("x", 0).wait_recv()
+    flow_all("y", 0).wait_recv()
+    flow_send("far_x", 0)
+    flow_send("far_y", 0)
     all_small(1, lists).wait_recv()
     row_at = lax.broadcasted_iota(jnp.int32, (tokens, K), 0)
     gauss_at = lax.broadcasted_iota(jnp.int32, (gpt, K), 0)
@@ -249,7 +305,7 @@
         for q in range(batch):
             j = peer(g * batch + q)[0]
             for b in range(tiles):
-                at = lists[j, pl.ds(b, 1), :]
+                at = lists[j, pl.ds(b, 1), :] // gpt
                 where[n, :, (q * tiles + b) * K : (q * tiles + b + 1) * K] = jnp.where(
                     row_at == at, 1.0, 0.0
                 ).astype(BF16)
@@ -262,9 +318,18 @@
     @pl.loop(0, group)
     def _(j):
         for b in range(tiles):
-            at = lists[j, pl.ds(tiles + b, 1), :]
+            at = lists[j, pl.ds(b, 1), :]
+            at = at - (at // gpt) * gpt
             fits[j, :, b * K : (b + 1) * K] = jnp.where(gauss_at == at, 1.0, 0.0).astype(BF16)
 
+    line_all(2).wait_recv()
+    flow_send("x", 2)
+    flow_send("y", 2)
+    flow_all("x", 1).wait_recv()
+    flow_all("y", 1).wait_recv()
+    flow_send("far_x", 1)
+    flow_send("far_y", 1)
+    turn_line(sec, lo)
     all_small(2, given).wait_recv()
     picked = mm(gathered(given).astype(BF16), perm[...], NN)
     rows = [picked[p : p + 1] for p in range(PARAMS)]
@@ -372,47 +437,22 @@
             recv_sem=recv, device_id=to, device_id_type=MESH,
         )
 
-    @pl.loop(1, group)
+    @each_peer
     def _(i):
         push(0, grads, i, r_grad.at[me]).start()
 
-    @pl.loop(1, group)
-    def _(i):
-        push(1, losses, i, s_loss.at[1]).start()
-
-    nb = nsec - 1
-    ns = nlo - 1
-    for n in range(nb + ns):
-        norm_copy(1 + n, line, partner).wait_recv()
-    cut_rows = tok_rows // 2
-    far = []
-    for a, (s, _) in enumerate(beside):
-        for b, (_, l) in enumerate(below):
-            far.append((a, b, s, l))
-
-    def far_copies():
-        out = []
-        base = 1 + nb + ns
-        for m, (a, b, s, l) in enumerate(far):
-            down_line = pl.ds((sec * nlo + l) * nhi, nhi)
-            side_line = pl.ds((s * nlo + lo) * nhi, nhi)
-            first = pl.ds(0, cut_rows)
-            second = pl.ds(cut_rows, tok_rows - cut_rows)
-            for n, span, part, to in (
-                (base + 2 * m, down_line, first, (s, hi * nlo + lo, scene)),
-                (base + 2 * m + 1, side_line, second, (sec, hi * nlo + l, scene)),
-            ):
-                out.append(
-                    pltpu.make_async_remote_copy(
-                        src_ref=norms.at[span, part], dst_ref=norms.at[span, part],
-                        send_sem=s_norm.at[n], recv_sem=r_norm.at[n], device_id=to,
-                        device_id_type=MESH,
-                    )
-                )
-        return out
-
-    for copy in far_copies():
-        copy.start()
+    flow_all("x", 2).wait_recv()
+    flow_all("y", 2).wait_recv()
+    turn_line(1 - sec, lo)
+    turn_line(sec, 1 - lo)
+
+    def late_sends():
+        flow_send("far_x", 2)
+        flow_send("far_y", 2)
+
+        @each_peer
+        def _(i):
+            push(1, losses, i, s_loss.at[1]).start()
 
     def gather_batch(g, n):
         sides = []
@@ -446,8 +486,11 @@
     if ahead:
         dhead[...] = gather_batch(0, 0)
         for g in range(1, group // batch):
+            if g == LATE:
+                late_sends()
             dhead[...] += gather_batch(g, g)
     else:
+        late_sends()
         dhead[...] = jnp.zeros_like(dhead)
 
         @pl.loop(0, group // batch)
@@ -461,14 +504,14 @@
         device_id=partner, device_id_type=MESH,
     ).wait_recv()
     loss_mine[...] = jnp.broadcast_to(jnp.sum(losses[...], axis=0), loss_mine.shape)
-    for copy in far_copies():
-        copy.wait_recv()
+    for name in ("far_x", "far_y"):
+        for c in range(3):
+            flow_all(name, c).wait_recv()
+    turn_line(1 - sec, 1 - lo)
     loss_copy = pltpu.make_async_remote_copy(
         src_ref=loss_mine, dst_ref=loss_theirs, send_sem=s_loss.at[0], recv_sem=r_loss,
         device_id=partner, device_id_type=MESH,
     )
-    for n in range(nsec * nlo):
-        turn_line(n)
     dh = dhead[...].astype(BF16)
     dhead_rows = 256
     chunks = width // dhead_rows
@@ -483,7 +526,8 @@
 
     for n in range(chunks):
         span = slice(n * dhead_rows, (n + 1) * dhead_rows)
-        mine[span, :] = mm(turned[span, :], dh, NT).astype(BF16)
+        side = jnp.concatenate([turned[m, span] for m in range(nsec * nlo)], axis=1)
+        mine[span, :] = mm(side, dh, NT).astype(BF16)
         if n == 0:
             loss_copy.start()
         else:
@@ -493,11 +537,9 @@
     for n in range(chunks):
         part_copy(n).wait_recv()
         span = slice(n * dhead_rows, (n + 1) * dhead_rows)
-        grad_ref[span, :] = (mine[span, :].astype(F32) + theirs[span, :].astype(F32)).astype(BF16)
+        grad_ref[span, :] = mine[span, :].astype(F32) + theirs[span, :].astype(F32)
     loss_copy.wait_recv()
-    loss_ref[...] = jnp.broadcast_to(
-        jnp.sum(loss_mine[0:1] + loss_theirs[0:1], keepdims=True), loss_ref.shape
-    )
+    loss_ref[...] = jnp.sum(loss_mine[0:1] + loss_theirs[0:1], keepdims=True)
 
     loss_copy.wait_send()
     for n in range(chunks):
@@ -514,17 +556,31 @@
         src_ref=loss_all, dst_ref=loss_all, send_sem=s_grad.at[1], recv_sem=s_loss.at[1],
         device_id=partner, device_id_type=MESH,
     ).wait_send()
-    norm_copy(0, pl.ds(0, nhi - 1), partner).wait_send()
-    for n in range(nb + ns):
-        norm_copy(1 + n, line, partner).wait_send()
-    for copy in far_copies():
-        copy.wait_send()
+    line_all(1).wait_send()
+    line_all(2).wait_send()
+    for name in flows:
+        for c in range(3):
+            flow_all(name, c).wait_send()
+
+
+def store(image_ref, grad_ref, loss_ref, image_out, grad_out, loss_out, sems):
+    pairs = [(image_ref, image_out), (loss_ref, loss_out)]
+    rows = grad_ref.shape[0] // STORES
+    for n in range(STORES):
+        span = pl.ds(n * rows, rows)
+        pairs.append((grad_ref.at[span], grad_out.at[span]))
+    copies = [pltpu.make_async_copy(src, dst, sems.at[n]) for n, (src, dst) in enumerate(pairs)]
+    for copy in copies:
+        copy.start()
+    for copy in copies:
+        copy.wait()
 
 
 def solution(mesh):
     nsec, nview, nscene = mesh.shape["section"], mesh.shape["view"], mesh.shape["scene"]
     group = nsec * nview
-    nlo = 2 if nview % 2 == 0 else 1
+    nlo = 2
+    assert nsec == 2 and nview % 8 == 0
 
     def body(tokens, norm_gain, head_weight, tile_lists, tile_counts, cameras, targets):
         tok_rows, width = tokens.shape[1:]
@@ -537,17 +593,16 @@
         factor = 1.0 / (nscene * tiles * group)
         ahead = group * group * tok_rows * slots <= 2**24
         batch = min(BATCH, group)
-        flows = 1 + (nsec - 1) + (nlo - 1) + 2 * (nsec - 1) * (nlo - 1)
         vmem = pl.BlockSpec(memory_space=pltpu.VMEM)
         smem = pl.BlockSpec(memory_space=pltpu.SMEM)
-        hbm = pl.BlockSpec(memory_space=pl.ANY)
+        hbm = pl.BlockSpec(memory_space=pltpu.HBM)
         dma = pltpu.SemaphoreType.DMA
         image, grad, loss = pl.pallas_call(
             functools.partial(kernel, nsec, nview, factor),
             out_shape=(
-                jax.ShapeDtypeStruct((tiles, targets.shape[2]), BF16),
-                jax.ShapeDtypeStruct((width, outw), BF16),
-                jax.ShapeDtypeStruct((8, 128), F32),
+                pltpu.VMEM((tiles, targets.shape[2]), BF16),
+                pltpu.VMEM((width, outw), F32),
+                pltpu.VMEM((1, 1), F32),
             ),
             in_specs=[hbm, hbm, hbm, hbm, smem, smem, hbm],
             out_specs=(vmem, vmem, vmem),
@@ -558,17 +613,17 @@
                 pltpu.VMEM((tiles, K), jnp.int32),
                 pltpu.VMEM((tiles, targets.shape[2]), BF16),
                 pltpu.VMEM((group * cap, slots), BF16),
-                pltpu.VMEM((packs, 8, 128), F32),
-                pltpu.VMEM((group, 8, 128), F32),
-                pltpu.VMEM((packs, 8, 128), F32),
-                pltpu.VMEM((group, 8, 128), F32),
-                pltpu.VMEM((group, 2 * tiles, K), jnp.int32),
+                pltpu.VMEM((packs, 1, 128), F32),
+                pltpu.VMEM((group, 1, 128), F32),
+                pltpu.VMEM((packs, PARAMS, 128), BF16),
+                pltpu.VMEM((group, PARAMS, 128), BF16),
+                pltpu.VMEM((group, tiles, K), jnp.int32),
                 pltpu.VMEM((group // batch if ahead else 1, group * tok_rows, batch * slots), BF16),
                 pltpu.VMEM((group, gpt, slots), BF16),
                 pltpu.VMEM((group, tok_rows, width), BF16),
                 pltpu.VMEM((group, 2 * PARAMS, slots // 2), BF16),
                 pltpu.VMEM((outw, group * tok_rows), F32),
-                pltpu.VMEM((width, group * tok_rows), BF16),
+                pltpu.VMEM((nsec * nlo, width, group * tok_rows // (nsec * nlo)), BF16),
                 pltpu.VMEM((width, outw), BF16),
                 pltpu.VMEM((width, outw), BF16),
                 pltpu.VMEM((group, 1, K), F32),
@@ -576,19 +631,29 @@
                 pltpu.VMEM((8, K), F32),
                 dma((5,)),
                 dma((3,)), dma((3,)),
-                dma((flows,)), dma((flows,)),
+                dma((15,)), dma((15,)),
                 dma((2,)), dma((group,)),
                 dma((width // 256,)), dma((width // 256,)),
                 dma((2,)), dma,
             ],
             compiler_params=pltpu.CompilerParams(
-                collective_id=0, has_side_effects=True, vmem_limit_bytes=60 * 1024 * 1024
+                collective_id=0, has_side_effects=True, vmem_limit_bytes=61 * 1024 * 1024
             ),
         )(
             tokens[0], norm_gain[None], head_weight, tile_lists[0], tile_counts[0], cameras[0],
             targets[0],
         )
-        return image[None], grad.astype(F32), loss[0, 0]
+        image, grad, loss = pl.pallas_call(
+            store,
+            out_shape=tuple(
+                jax.ShapeDtypeStruct(x.shape, x.dtype) for x in (image, grad, loss)
+            ),
+            in_specs=[vmem] * 3,
+            out_specs=(hbm,) * 3,
+            scratch_shapes=[dma((2 + STORES,))],
+            compiler_params=pltpu.CompilerParams(vmem_limit_bytes=1024 * 1024),
+        )(image, grad, loss)
+        return image[None], grad, loss[0, 0]
 
     in_specs = (
         P("scene", ("section", "view"), None),

time: 40.1 us -> 33.9 us (0.85)
  other arithmetic: 2.83 us -> 0 us
  local copies, waits for them, and re-layouts: 1.79 us -> 0 us
  Pallas kernels: 34.6 us -> 33 us
    pallas_call x1, Pallas kernels: 34.6 us -> 31.1 us  [body(): pl.pallas_call(functools.partial(kernel, nsec, nview, factor), out_shape=...]
    convert_element_type x1 -> x0, other arithmetic: 2.83 us -> none  [body(): return (image[None], grad.astype(F32), loss[0, 0])]
    pallas_call x0 -> x1, Pallas kernels: none -> 1.99 us  [body(): pl.pallas_call(store, out_shape=tuple((jax.ShapeDtypeStruct(x.shape, x.dt...]
    slice x1 -> x0, local copies, waits for them, and re-layouts: 1.2 us -> none  [body(): return (image[None], grad.astype(F32), loss[0, 0])]
    unnamed x3 -> x0, local copies, waits for them, and re-layouts: 0.6 us -> none
where the time goes in v3:
time: 33.9 us; the launch traced here: 33.7 us
  Pallas kernels  33 us (97%)
  between operations  0.64 us (2%)
    pallas_call x1, Pallas kernels, body(): pl.pallas_call(functools.partial(kernel, nsec, nview, factor), out_shape=...  31.1 us
    pallas_call x1, Pallas kernels, body(): pl.pallas_call(store, out_shape=tuple((jax.ShapeDtypeStruct(x.shape, x.dt...  1.99 us

profile of v3, /device:TPU:1, one launch (start us, length us, event | category | flops | bytes accessed | tf_op | source)
XLA Modules:
  0.0 33.7 jit_solution(9829049058021635761)
XLA Ops:
  0.6 31.1 %shard_map.94 = (bf16[4,768]{1,0:T(4,128)(2,1)S(1)}, f32[1024,512]{1,0:T(8,128)S(1)}, f32[1,1]{1,0:T(1,128)}) custom-call(bf16[32,1024]{1,0:T(8,128)(2,1)} %bitcast.8, f32[1,1024]{1,0:T(1,128)} %bitcast.10, bf16[1024,512]{1,0:T(8,128)(2,1)} %w_hbm.1, s32[4,128]{1,0:T(4,128)} %bitcast.11, s32[4]{0:T(128)} %bitcast.13, f32[2,8]{1,0:T(2,128)} %bitcast.12, ...), custom_call_target="tpu_custom_call" | custom-call | tf_op jit(solution)/shard_map/pallas_call | solution.py:600
  31.7 2.0 %shard_map.95 = (bf16[4,768]{1,0:T(4,128)(2,1)}, f32[1024,512]{1,0:T(8,128)}, f32[1,1]{1,0:T(1,128)}) custom-call(bf16[4,768]{1,0:T(4,128)(2,1)S(1)} %get-tuple-element.9.image_ref, f32[1024,512]{1,0:T(8,128)S(1)} %get-tuple-element.10.grad_ref, f32[1,1]{1,0:T(1,128)} %get-tuple-element.11.loss_ref), custom_call_target="tpu_custom_call" | custom-call | tf_op jit(solution)/shard_map/pallas_call | solution.py:646

commit v4 on v3

--- a/solution.py
+++ b/solution.py
@@ -8,9 +8,10 @@
 from jax.sharding import PartitionSpec as P
 
 PARAMS = 8
+ROWS = 7
 SIDE = 16
 BATCH = 2
-STORES = 1
+FINISH = 0
 LATE = 1
 VIEWS = 2
 MESH = pl.DeviceIdType.MESH
@@ -58,9 +59,9 @@
     tok_hbm, gain_hbm, w_hbm, list_hbm, count_ref, cam_ref, want_hbm,
     image_ref, grad_ref, loss_ref,
     tok_ref, gain_ref, w_ref, list_ref, want_ref,
-    perm, asked, wanted, found, given, lists, where, fits, norms, grads, dhead, turned, mine, theirs,
+    perm, asked, wanted, found, given, lists, where, fits, norms, grads, dhead, turned, turned_far, mine, theirs,
     losses, loss_mine, loss_theirs,
-    s_in, s_small, r_small, s_norm, r_norm, s_grad, r_grad, s_part, r_part, s_loss, r_loss,
+    s_in, s_small, r_small, s_norm, r_norm, s_grad, r_grad, s_part, r_part, s_loss, r_loss, s_turn, r_turn,
 ):
     group = nsec * nview
     nlo = 2
@@ -286,9 +287,17 @@
 
     stretch = nhi * tok_rows
 
-    def turn_line(s, l):
+    def turn_copy(m, s, l):
+        n = s * nlo + l
+        return pltpu.make_async_remote_copy(
+            src_ref=turned.at[n], dst_ref=turned_far.at[n], send_sem=s_turn.at[m],
+            recv_sem=r_turn.at[m], device_id=partner, device_id_type=MESH,
+        )
+
+    def turn_line(m, s, l):
         n = s * nlo + l
         turned[n] = norms[pl.ds(n * nhi, nhi)].reshape(stretch, width).T
+        turn_copy(m, s, l).start()
 
     line_all(1).wait_recv()
     flow_send("x", 1)
@@ -301,9 +310,12 @@
     row_at = lax.broadcasted_iota(jnp.int32, (tokens, K), 0)
     gauss_at = lax.broadcasted_iota(jnp.int32, (gpt, K), 0)
 
+    def source(g, q):
+        return (g // 2) * (2 * batch) + g % 2 + 2 * q
+
     def mark_rows(g, n):
         for q in range(batch):
-            j = peer(g * batch + q)[0]
+            j = peer(source(g, q))[0]
             for b in range(tiles):
                 at = lists[j, pl.ds(b, 1), :] // gpt
                 where[n, :, (q * tiles + b) * K : (q * tiles + b + 1) * K] = jnp.where(
@@ -329,7 +341,7 @@
     flow_all("y", 1).wait_recv()
     flow_send("far_x", 1)
     flow_send("far_y", 1)
-    turn_line(sec, lo)
+    turn_line(0, sec, lo)
     all_small(2, given).wait_recv()
     picked = mm(gathered(given).astype(BF16), perm[...], NN)
     rows = [picked[p : p + 1] for p in range(PARAMS)]
@@ -346,8 +358,8 @@
         [jnp.ones((1, pix), F32), across, down, across * across + down * down, jnp.zeros((4, pix), F32)],
         axis=0,
     ).astype(BF16)
-    vi = me * VIEWS // group
-    cam = [cam_ref[vi, n] for n in range(8)]
+    cam = [cam_ref[sec, n] for n in range(8)]
+    cam_far = [cam_ref[1 - sec, n] for n in range(8)]
     slot = lax.broadcasted_iota(jnp.int32, (1, K), 1)
     live = jnp.concatenate(
         [jnp.where(slot < count_ref[b], 1.0, 0.0) for b in range(tiles)], axis=1
@@ -418,12 +430,12 @@
     py = spread * s_y * (1.0 - sy * sy)
     out = jnp.concatenate(
         [
-            cam[0] * px + cam[4] * py,
-            cam[1] * px + cam[5] * py,
-            cam[2] * px + cam[6] * py,
+            px,
+            py,
             spread * s_r,
             (1.0 - sop) * s_h,
             dshade[0:3] * shade * (1.0 - shade),
+            jnp.zeros((1, slots), F32),
         ],
         axis=0,
     )
@@ -443,8 +455,8 @@
 
     flow_all("x", 2).wait_recv()
     flow_all("y", 2).wait_recv()
-    turn_line(1 - sec, lo)
-    turn_line(sec, 1 - lo)
+    turn_line(1, 1 - sec, lo)
+    turn_line(2, sec, 1 - lo)
 
     def late_sends():
         flow_send("far_x", 2)
@@ -457,7 +469,7 @@
     def gather_batch(g, n):
         sides = []
         for q in range(batch):
-            i = g * batch + q
+            i = source(g, q)
             j = peer(i)[0]
             if isinstance(i, int):
                 if i > 0:
@@ -476,27 +488,42 @@
                             ],
                             axis=1,
                         )
-                        for p in range(PARAMS)
+                        for p in range(ROWS)
                     ],
                     axis=0,
                 )
             )
         return mm(jnp.concatenate(sides, axis=1), where[n], NT)
 
+    def finish_turning():
+        for name in ("far_x", "far_y"):
+            for c in range(3):
+                flow_all(name, c).wait_recv()
+        turn_line(3, 1 - sec, 1 - lo)
+
+    last = group // batch - 1
     if ahead:
-        dhead[...] = gather_batch(0, 0)
-        for g in range(1, group // batch):
+        for g in range(last + 1):
             if g == LATE:
                 late_sends()
-            dhead[...] += gather_batch(g, g)
+            if g == last + FINISH:
+                finish_turning()
+            if g < 2:
+                dhead[g] = gather_batch(g, g)
+            else:
+                dhead[g % 2] += gather_batch(g, g)
+        if FINISH > 0:
+            finish_turning()
     else:
         late_sends()
         dhead[...] = jnp.zeros_like(dhead)
 
-        @pl.loop(0, group // batch)
+        @pl.loop(0, last + 1)
         def _(g):
             mark_rows(g, 0)
-            dhead[...] += gather_batch(g, 0)
+            dhead[g % 2] += gather_batch(g, 0)
+
+        finish_turning()
 
     loss_all = losses.at[pl.ds(0, group - 1)]
     pltpu.make_async_remote_copy(
@@ -504,46 +531,65 @@
         device_id=partner, device_id_type=MESH,
     ).wait_recv()
     loss_mine[...] = jnp.broadcast_to(jnp.sum(losses[...], axis=0), loss_mine.shape)
-    for name in ("far_x", "far_y"):
-        for c in range(3):
-            flow_all(name, c).wait_recv()
-    turn_line(1 - sec, 1 - lo)
     loss_copy = pltpu.make_async_remote_copy(
         src_ref=loss_mine, dst_ref=loss_theirs, send_sem=s_loss.at[0], recv_sem=r_loss,
         device_id=partner, device_id_type=MESH,
     )
-    dh = dhead[...].astype(BF16)
+    chunk = outw // 2
     dhead_rows = 256
     chunks = width // dhead_rows
 
-    def part_copy(n):
-        span = pl.ds(n * dhead_rows, dhead_rows)
+    def part_copy(c):
+        span = pl.ds(c * chunk, chunk)
         return pltpu.make_async_remote_copy(
             src_ref=mine.at[span], dst_ref=theirs.at[span],
-            send_sem=s_part.at[n], recv_sem=r_part.at[n],
+            send_sem=s_part.at[c], recv_sem=r_part.at[c],
             device_id=partner, device_id_type=MESH,
         )
 
+    def share(v, n):
+        return dhead[v, n * gpt : (n + 1) * gpt]
+
+    for p in range(PARAMS):
+        if p < 3:
+            value = (
+                cam[p] * share(0, 0) + cam[p + 4] * share(0, 1)
+                + cam_far[p] * share(1, 0) + cam_far[p + 4] * share(1, 1)
+            )
+        else:
+            value = share(0, p - 1) + share(1, p - 1)
+        mine[p * gpt : (p + 1) * gpt] = value.astype(BF16)
+        if (p + 1) * gpt % chunk == 0:
+            part_copy((p + 1) * gpt // chunk - 1).start()
+    loss_copy.start()
+
+    def sides(buf, n):
+        span = slice(n * dhead_rows, (n + 1) * dhead_rows)
+        return span, jnp.concatenate([buf[m, span] for m in range(nsec * nlo)], axis=1)
+
+    dh = mine[...]
     for n in range(chunks):
-        span = slice(n * dhead_rows, (n + 1) * dhead_rows)
-        side = jnp.concatenate([turned[m, span] for m in range(nsec * nlo)], axis=1)
-        mine[span, :] = mm(side, dh, NT).astype(BF16)
-        if n == 0:
-            loss_copy.start()
-        else:
-            part_copy(n - 1).start()
-    part_copy(chunks - 1).start()
-
-    for n in range(chunks):
-        part_copy(n).wait_recv()
-        span = slice(n * dhead_rows, (n + 1) * dhead_rows)
-        grad_ref[span, :] = mine[span, :].astype(F32) + theirs[span, :].astype(F32)
+        span, side = sides(turned, n)
+        grad_ref[span, :] = mm(side, dh, NT)
+    for m in range(nsec * nlo):
+        turn_copy(m, 0, 0).wait_recv()
+    for c in range(2):
+        part_copy(c).wait_recv()
+        cut = slice(c * chunk, (c + 1) * chunk)
+        dh = theirs[cut]
+        for n in range(chunks):
+            span, side = sides(turned_far, n)
+            grad_ref[span, cut] += mm(side, dh, NT)
     loss_copy.wait_recv()
-    loss_ref[...] = jnp.sum(loss_mine[0:1] + loss_theirs[0:1], keepdims=True)
+    loss_ref[...] = jnp.broadcast_to(
+        jnp.sum(loss_mine[0:1] + loss_theirs[0:1], keepdims=True), loss_ref.shape
+    )
 
     loss_copy.wait_send()
-    for n in range(chunks):
-        part_copy(n).wait_send()
+    for c in range(2):
+        part_copy(c).wait_send()
+    for m in range(nsec * nlo):
+        turn_copy(m, 0, 0).wait_send()
     all_small(0, wanted).wait_send()
     all_small(1, lists).wait_send()
     all_small(2, given).wait_send()
@@ -563,13 +609,10 @@
             flow_all(name, c).wait_send()
 
 
-def store(image_ref, grad_ref, loss_ref, image_out, grad_out, loss_out, sems):
-    pairs = [(image_ref, image_out), (loss_ref, loss_out)]
-    rows = grad_ref.shape[0] // STORES
-    for n in range(STORES):
-        span = pl.ds(n * rows, rows)
-        pairs.append((grad_ref.at[span], grad_out.at[span]))
+def store(image_ref, grad_ref, loss_ref, image_out, grad_out, loss_out, one, sems):
+    pairs = [(grad_ref, grad_out), (image_ref, image_out), (one, loss_out)]
     copies = [pltpu.make_async_copy(src, dst, sems.at[n]) for n, (src, dst) in enumerate(pairs)]
+    one[...] = loss_ref[0:1, 0:1]
     for copy in copies:
         copy.start()
     for copy in copies:
@@ -602,7 +645,7 @@
             out_shape=(
                 pltpu.VMEM((tiles, targets.shape[2]), BF16),
                 pltpu.VMEM((width, outw), F32),
-                pltpu.VMEM((1, 1), F32),
+                pltpu.VMEM((8, 128), F32),
             ),
             in_specs=[hbm, hbm, hbm, hbm, smem, smem, hbm],
             out_specs=(vmem, vmem, vmem),
@@ -622,10 +665,11 @@
                 pltpu.VMEM((group, gpt, slots), BF16),
                 pltpu.VMEM((group, tok_rows, width), BF16),
                 pltpu.VMEM((group, 2 * PARAMS, slots // 2), BF16),
-                pltpu.VMEM((outw, group * tok_rows), F32),
+                pltpu.VMEM((2, ROWS * gpt, group * tok_rows), F32),
                 pltpu.VMEM((nsec * nlo, width, group * tok_rows // (nsec * nlo)), BF16),
-                pltpu.VMEM((width, outw), BF16),
-                pltpu.VMEM((width, outw), BF16),
+                pltpu.VMEM((nsec * nlo, width, group * tok_rows // (nsec * nlo)), BF16),
+                pltpu.VMEM((outw, group * tok_rows), BF16),
+                pltpu.VMEM((outw, group * tok_rows), BF16),
                 pltpu.VMEM((group, 1, K), F32),
                 pltpu.VMEM((8, K), F32),
                 pltpu.VMEM((8, K), F32),
@@ -633,8 +677,9 @@
                 dma((3,)), dma((3,)),
                 dma((15,)), dma((15,)),
                 dma((2,)), dma((group,)),
-                dma((width // 256,)), dma((width // 256,)),
+                dma((2,)), dma((2,)),
                 dma((2,)), dma,
+                dma((nsec * nlo,)), dma((nsec * nlo,)),
             ],
             compiler_params=pltpu.CompilerParams(
                 collective_id=0, has_side_effects=True, vmem_limit_bytes=61 * 1024 * 1024
@@ -646,11 +691,12 @@
         image, grad, loss = pl.pallas_call(
             store,
             out_shape=tuple(
-                jax.ShapeDtypeStruct(x.shape, x.dtype) for x in (image, grad, loss)
+                jax.ShapeDtypeStruct(shape, dtype)
+                for shape, dtype in ((image.shape, BF16), (grad.shape, F32), ((1, 1), F32))
             ),
             in_specs=[vmem] * 3,
             out_specs=(hbm,) * 3,
-            scratch_shapes=[dma((2 + STORES,))],
+            scratch_shapes=[pltpu.VMEM((1, 1), F32), dma((3,))],
             compiler_params=pltpu.CompilerParams(vmem_limit_bytes=1024 * 1024),
         )(image, grad, loss)
         return image[None], grad, loss[0, 0]

time: 33.9 us -> 32.1 us (0.947)
  Pallas kernels: 33 us -> 31.3 us
    pallas_call x1, Pallas kernels: 31.1 us -> 30 us  [body(): pl.pallas_call(functools.partial(kernel, nsec, nview, factor), out_shape=...]
    pallas_call x1, Pallas kernels: 1.99 us -> 1.35 us  [body(): pl.pallas_call(store, out_shape=tuple((jax.ShapeDtypeStruct(shape, dtype)...]
where the time goes in v4:
time: 32.1 us; the launch traced here: 32 us
  Pallas kernels  31.3 us (98%)
  between operations  0.64 us (2%)
    pallas_call x1, Pallas kernels, body(): pl.pallas_call(functools.partial(kernel, nsec, nview, factor), out_shape=...  30 us
    pallas_call x1, Pallas kernels, body(): pl.pallas_call(store, out_shape=tuple((jax.ShapeDtypeStruct(shape, dtype)...  1.35 us

profile of v4, /device:TPU:1, one launch (start us, length us, event | category | flops | bytes accessed | tf_op | source)
XLA Modules:
  0.0 32.0 jit_solution(4395060553418513338)
XLA Ops:
  0.6 30.0 %shard_map.94 = (bf16[4,768]{1,0:T(4,128)(2,1)S(1)}, f32[1024,512]{1,0:T(8,128)S(1)}, f32[8,128]{1,0:T(8,128)S(1)}) custom-call(bf16[32,1024]{1,0:T(8,128)(2,1)} %bitcast.8, f32[1,1024]{1,0:T(1,128)} %bitcast.10, bf16[1024,512]{1,0:T(8,128)(2,1)} %w_hbm.1, s32[4,128]{1,0:T(4,128)} %bitcast.11, s32[4]{0:T(128)} %bitcast.13, f32[2,8]{1,0:T(2,128)} %bitcast.12, ...), custom_call_target="tpu_custom_call" | custom-call | tf_op jit(solution)/shard_map/pallas_call | solution.py:643
  30.6 1.4 %shard_map.95 = (bf16[4,768]{1,0:T(4,128)(2,1)}, f32[1024,512]{1,0:T(8,128)}, f32[1,1]{1,0:T(1,128)}) custom-call(bf16[4,768]{1,0:T(4,128)(2,1)S(1)} %get-tuple-element.9.image_ref, f32[1024,512]{1,0:T(8,128)S(1)} %get-tuple-element.10.grad_ref, f32[8,128]{1,0:T(8,128)S(1)} %get-tuple-element.11.loss_ref), custom_call_target="tpu_custom_call" | custom-call | tf_op jit(solution)/shard_map/pallas_call | solution.py:691

commit v5 on v4

--- a/solution.py
+++ b/solution.py
@@ -11,6 +11,7 @@
 ROWS = 7
 SIDE = 16
 BATCH = 2
+STORES = 1
 FINISH = 0
 LATE = 1
 VIEWS = 2
@@ -203,7 +204,7 @@
 
     def norm_copy(n, ref, to):
         return pltpu.make_async_remote_copy(
-            src_ref=ref, dst_ref=ref, send_sem=s_norm.at[n], recv_sem=r_norm.at[n],
+            src_ref=ref, dst_ref=ref, send_sem=s_norm, recv_sem=r_norm.at[n],
             device_id=to, device_id_type=MESH,
         )
 
@@ -287,17 +288,17 @@
 
     stretch = nhi * tok_rows
 
-    def turn_copy(m, s, l):
+    def turn_copy(s, l):
         n = s * nlo + l
         return pltpu.make_async_remote_copy(
-            src_ref=turned.at[n], dst_ref=turned_far.at[n], send_sem=s_turn.at[m],
-            recv_sem=r_turn.at[m], device_id=partner, device_id_type=MESH,
+            src_ref=turned.at[n], dst_ref=turned_far.at[n], send_sem=s_turn,
+            recv_sem=r_turn, device_id=partner, device_id_type=MESH,
         )
 
-    def turn_line(m, s, l):
+    def turn_line(s, l):
         n = s * nlo + l
         turned[n] = norms[pl.ds(n * nhi, nhi)].reshape(stretch, width).T
-        turn_copy(m, s, l).start()
+        turn_copy(s, l).start()
 
     line_all(1).wait_recv()
     flow_send("x", 1)
@@ -341,7 +342,7 @@
     flow_all("y", 1).wait_recv()
     flow_send("far_x", 1)
     flow_send("far_y", 1)
-    turn_line(0, sec, lo)
+    turn_line(sec, lo)
     all_small(2, given).wait_recv()
     picked = mm(gathered(given).astype(BF16), perm[...], NN)
     rows = [picked[p : p + 1] for p in range(PARAMS)]
@@ -455,8 +456,8 @@
 
     flow_all("x", 2).wait_recv()
     flow_all("y", 2).wait_recv()
-    turn_line(1, 1 - sec, lo)
-    turn_line(2, sec, 1 - lo)
+    turn_line(1 - sec, lo)
+    turn_line(sec, 1 - lo)
 
     def late_sends():
         flow_send("far_x", 2)
@@ -499,7 +500,7 @@
         for name in ("far_x", "far_y"):
             for c in range(3):
                 flow_all(name, c).wait_recv()
-        turn_line(3, 1 - sec, 1 - lo)
+        turn_line(1 - sec, 1 - lo)
 
     last = group // batch - 1
     if ahead:
@@ -550,7 +551,7 @@
     def share(v, n):
         return dhead[v, n * gpt : (n + 1) * gpt]
 
-    for p in range(PARAMS):
+    for p in [4, 5, 6, 7, 0, 1, 2, 3]:
         if p < 3:
             value = (
                 cam[p] * share(0, 0) + cam[p + 4] * share(0, 1)
@@ -571,9 +572,12 @@
     for n in range(chunks):
         span, side = sides(turned, n)
         grad_ref[span, :] = mm(side, dh, NT)
-    for m in range(nsec * nlo):
-        turn_copy(m, 0, 0).wait_recv()
-    for c in range(2):
+    turn_all = pltpu.make_async_remote_copy(
+        src_ref=turned, dst_ref=turned_far, send_sem=s_turn, recv_sem=r_turn,
+        device_id=partner, device_id_type=MESH,
+    )
+    turn_all.wait_recv()
+    for c in (1, 0):
         part_copy(c).wait_recv()
         cut = slice(c * chunk, (c + 1) * chunk)
         dh = theirs[cut]
@@ -588,8 +592,7 @@
     loss_copy.wait_send()
     for c in range(2):
         part_copy(c).wait_send()
-    for m in range(nsec * nlo):
-        turn_copy(m, 0, 0).wait_send()
+    turn_all.wait_send()
     all_small(0, wanted).wait_send()
     all_small(1, lists).wait_send()
     all_small(2, given).wait_send()
@@ -602,15 +605,15 @@
         src_ref=loss_all, dst_ref=loss_all, send_sem=s_grad.at[1], recv_sem=s_loss.at[1],
         device_id=partner, device_id_type=MESH,
     ).wait_send()
-    line_all(1).wait_send()
-    line_all(2).wait_send()
-    for name in flows:
-        for c in range(3):
-            flow_all(name, c).wait_send()
+    norm_copy(0, norms.at[pl.ds(0, group - 1)], partner).wait_send()
 
 
 def store(image_ref, grad_ref, loss_ref, image_out, grad_out, loss_out, one, sems):
-    pairs = [(grad_ref, grad_out), (image_ref, image_out), (one, loss_out)]
+    rows = grad_ref.shape[0] // STORES
+    pairs = [(image_ref, image_out), (one, loss_out)]
+    for n in range(STORES):
+        span = pl.ds(n * rows, rows)
+        pairs.append((grad_ref.at[span], grad_out.at[span]))
     copies = [pltpu.make_async_copy(src, dst, sems.at[n]) for n, (src, dst) in enumerate(pairs)]
     one[...] = loss_ref[0:1, 0:1]
     for copy in copies:
@@ -675,11 +678,11 @@
                 pltpu.VMEM((8, K), F32),
                 dma((5,)),
                 dma((3,)), dma((3,)),
-                dma((15,)), dma((15,)),
+                dma, dma((15,)),
                 dma((2,)), dma((group,)),
                 dma((2,)), dma((2,)),
                 dma((2,)), dma,
-                dma((nsec * nlo,)), dma((nsec * nlo,)),
+                dma, dma,
             ],
             compiler_params=pltpu.CompilerParams(
                 collective_id=0, has_side_effects=True, vmem_limit_bytes=61 * 1024 * 1024
@@ -696,7 +699,7 @@
             ),
             in_specs=[vmem] * 3,
             out_specs=(hbm,) * 3,
-            scratch_shapes=[pltpu.VMEM((1, 1), F32), dma((3,))],
+            scratch_shapes=[pltpu.VMEM((1, 1), F32), dma((2 + STORES,))],
             compiler_params=pltpu.CompilerParams(vmem_limit_bytes=1024 * 1024),
         )(image, grad, loss)
         return image[None], grad, loss[0, 0]

time: 32.1 us -> 31.8 us (level)
  no operation moved by 1% of the time
where the time goes in v5:
time: 31.8 us; the launch traced here: 31.7 us
  Pallas kernels  31 us (97%)
  between operations  0.64 us (2%)
    pallas_call x1, Pallas kernels, body(): pl.pallas_call(functools.partial(kernel, nsec, nview, factor), out_shape=...  29.7 us
    pallas_call x1, Pallas kernels, body(): pl.pallas_call(store, out_shape=tuple((jax.ShapeDtypeStruct(shape, dtype)...  1.36 us

profile of v5, /device:TPU:1, one launch (start us, length us, event | category | flops | bytes accessed | tf_op | source)
XLA Modules:
  0.0 31.7 jit_solution(12016629675244086889)
XLA Ops:
  0.6 29.7 %shard_map.94 = (bf16[4,768]{1,0:T(4,128)(2,1)S(1)}, f32[1024,512]{1,0:T(8,128)S(1)}, f32[8,128]{1,0:T(8,128)S(1)}) custom-call(bf16[32,1024]{1,0:T(8,128)(2,1)} %bitcast.8, f32[1,1024]{1,0:T(1,128)} %bitcast.10, bf16[1024,512]{1,0:T(8,128)(2,1)} %w_hbm.1, s32[4,128]{1,0:T(4,128)} %bitcast.11, s32[4]{0:T(128)} %bitcast.13, f32[2,8]{1,0:T(2,128)} %bitcast.12, ...), custom_call_target="tpu_custom_call" | custom-call | tf_op jit(solution)/shard_map/pallas_call | solution.py:646
  30.3 1.4 %shard_map.95 = (bf16[4,768]{1,0:T(4,128)(2,1)}, f32[1024,512]{1,0:T(8,128)}, f32[1,1]{1,0:T(1,128)}) custom-call(bf16[4,768]{1,0:T(4,128)(2,1)S(1)} %get-tuple-element.9.image_ref, f32[1024,512]{1,0:T(8,128)S(1)} %get-tuple-element.10.grad_ref, f32[8,128]{1,0:T(8,128)S(1)} %get-tuple-element.11.loss_ref), custom_call_target="tpu_custom_call" | custom-call | tf_op jit(solution)/shard_map/pallas_call | solution.py:694

commit v6 on v5

--- a/solution.py
+++ b/solution.py
@@ -13,7 +13,7 @@
 BATCH = 2
 STORES = 1
 FINISH = 0
-LATE = 1
+LATE = 0
 VIEWS = 2
 MESH = pl.DeviceIdType.MESH
 F32 = jnp.float32

time: 31.8 us -> 31.7 us (level)
  no operation moved by 1% of the time
where the time goes in v6:
time: 31.7 us; the launch traced here: 31.6 us
  Pallas kernels  30.9 us (97%)
  between operations  0.64 us (2%)
    pallas_call x1, Pallas kernels, body(): pl.pallas_call(functools.partial(kernel, nsec, nview, factor), out_shape=...  29.6 us
    pallas_call x1, Pallas kernels, body(): pl.pallas_call(store, out_shape=tuple((jax.ShapeDtypeStruct(shape, dtype)...  1.36 us

profile of v6, /device:TPU:1, one launch (start us, length us, event | category | flops | bytes accessed | tf_op | source)
XLA Modules:
  0.0 31.6 jit_solution(18409072266336015286)
XLA Ops:
  0.6 29.6 %shard_map.94 = (bf16[4,768]{1,0:T(4,128)(2,1)S(1)}, f32[1024,512]{1,0:T(8,128)S(1)}, f32[8,128]{1,0:T(8,128)S(1)}) custom-call(bf16[32,1024]{1,0:T(8,128)(2,1)} %bitcast.8, f32[1,1024]{1,0:T(1,128)} %bitcast.10, bf16[1024,512]{1,0:T(8,128)(2,1)} %w_hbm.1, s32[4,128]{1,0:T(4,128)} %bitcast.11, s32[4]{0:T(128)} %bitcast.13, f32[2,8]{1,0:T(2,128)} %bitcast.12, ...), custom_call_target="tpu_custom_call" | custom-call | tf_op jit(solution)/shard_map/pallas_call | solution.py:646
  30.2 1.4 %shard_map.95 = (bf16[4,768]{1,0:T(4,128)(2,1)}, f32[1024,512]{1,0:T(8,128)}, f32[1,1]{1,0:T(1,128)}) custom-call(bf16[4,768]{1,0:T(4,128)(2,1)S(1)} %get-tuple-element.9.image_ref, f32[1024,512]{1,0:T(8,128)S(1)} %get-tuple-element.10.grad_ref, f32[8,128]{1,0:T(8,128)S(1)} %get-tuple-element.11.loss_ref), custom_call_target="tpu_custom_call" | custom-call | tf_op jit(solution)/shard_map/pallas_call | solution.py:694
